TPU v7x, 32 devices: a whole 2x2x4 slice. The times are simulated.
32 devices in a mesh: blk: 8 (over y, x, core), rep: 4 (over z).
Axes of the slice: x: 2, y: 2, z: 4, core: 2. Of those that a mesh axis runs over, the one named last changes fastest.
Arguments:
- anchors: float32 [3, 8192], P(None, ('blk', 'rep')), may hold values from -1 to 1
- directions: float32 [3, 8192], P(None, ('blk', 'rep')), may hold values from -4 to 4
- app_ids: int32 [8192], P(('blk', 'rep')), may hold values from 0 to 8191
- block_ids: int32 [64, 3], P(('blk', 'rep')), may hold values from 0 to 7, as said below
- color_grad: float32 [3, 8192], P(None, ('blk', 'rep')), may hold values from -6 to 6
- block_centers: float32 [3, 8], P(None, 'blk'), may hold values from -1 to 1
- pos_weight: bfloat16 [8, 256, 63], P('blk'), may hold values from -1 to 1
- trunk_weight: bfloat16 [8, 2, 256, 256], P('blk'), may hold values from -0.5 to 0.5
- density_weight: bfloat16 [8, 256], P('blk'), may hold values from -0.5 to 0.5
- feature_weight: bfloat16 [8, 128, 256], P('blk'), may hold values from -0.5 to 0.5
- view_weight: bfloat16 [8, 128, 27], P('blk'), may hold values from -1.25 to 1.25
- code_weight: bfloat16 [8, 128, 32], P('blk'), may hold values from -1 to 1
- radiance_weight: bfloat16 [8, 3, 128], P('blk'), may hold values from -0.75 to 0.75
- code_table: bfloat16 [8, 32, 8192], P('blk'), may hold values from -5 to 5
Outputs:
- colors: float32 [3, 8192], P(None, ('blk', 'rep'))
- grad_pos_weight: float32 [8, 256, 63], P('blk')
- grad_trunk_weight: float32 [8, 2, 256, 256], P('blk')
- grad_density_weight: float32 [8, 256], P('blk')
- grad_feature_weight: float32 [8, 128, 256], P('blk')
- grad_view_weight: float32 [8, 128, 27], P('blk')
- grad_code_weight: float32 [8, 128, 32], P('blk')
- grad_radiance_weight: float32 [8, 3, 128], P('blk')
- grad_code_table: float32 [8, 32, 8192], P('blk')
Inputs may be any that keep to these rules, and one draw needn't show every extreme that they name: `block_ids`: each tile names three different blocks; the tiles of one device never name the same block twice; among the devices that share an index along rep, every block is named by at most 8 tiles, and some block by exactly 8 tiles.
All inputs are finite; a program needn't handle non-finite values.
Results may differ from a plain program's by a relative error of at most 0.015.
Values sent between devices are 32-bit elements; how exact they have to be, the bound alone decides.
No kernel may reach another device: no remote copies, remote signals or barrier semaphores. Data moves between devices by JAX's collectives and lax.ppermute only.
A program may use at most 64 MiB of HBM per device.

v0:
```python
import functools

import jax
import jax.numpy as jnp
from jax import lax
from jax.experimental import pallas as pl
from jax.experimental.pallas import tpu as pltpu
from jax.sharding import PartitionSpec as P


TILE = 128
SAMPLES = 4
FREQ = 10
VFREQ = 4
COLS = SAMPLES * TILE
LOW = 256
ROWS = 16
VCODE = 32
EDGE = 144
DENSE = 131

ray_span = 2.0
loss_scale = 0.03125
spacing = ray_span / SAMPLES

F32 = jnp.float32
BF16 = jnp.bfloat16


def dot(a, b):
    return lax.dot_general(a, b, (((1,), (0,)), ((), ())), preferred_element_type=F32)


def dot_nt(a, b):
    return lax.dot_general(a, b, (((1,), (1,)), ((), ())), preferred_element_type=F32)


def vmem():
    return pl.BlockSpec(memory_space=pltpu.VMEM)


def smem():
    return pl.BlockSpec(memory_space=pltpu.SMEM)


def whole(shape):
    return pl.BlockSpec(shape, lambda i: (0,) * len(shape))


def sin_cos(angle, is_cos):
    turns = jnp.floor(angle * 0.6366197723675814 + 0.5)
    rest = angle - turns * 1.5703125
    rest = rest - turns * 4.837512969970703125e-4
    rest = rest - turns * 7.54978995489188216e-8
    quarter = turns.astype(jnp.int32) + is_cos
    sq = rest * rest
    sine = rest + rest * sq * (
        -1.6666654611e-1 + sq * (8.3321608736e-3 + sq * -1.9515295891e-4)
    )
    cosine = (
        1.0
        - 0.5 * sq
        + sq * sq * (4.166664568298827e-2 + sq * (-1.388731625493765e-3 + sq * 2.443315711809948e-5))
    )
    value = jnp.where((quarter & 1) == 1, cosine, sine)
    return jnp.where((quarter & 2) == 2, -value, value)


def encode(coords, levels, rows):
    n = coords[0].shape[1]
    row = lax.broadcasted_iota(jnp.int32, (rows, n), 0)
    third = (row * 171) >> 9
    coord = row - 3 * third
    base = jnp.where(coord == 0, coords[0], jnp.where(coord == 1, coords[1], coords[2]))
    is_cos = (third > levels).astype(jnp.int32)
    level = jnp.clip(third - 1 - levels * is_cos, 0, levels - 1)
    scale = (1 << level).astype(F32)
    return jnp.where(third == 0, base, sin_cos(base * scale, is_cos))


def softplus(v):
    return jnp.maximum(v, 0.0) + jnp.log(1.0 + jnp.exp(-jnp.abs(v)))


def slope(h):
    return 1.0 - jnp.exp(-h.astype(F32))


def send_kernel(tiles, ids_ref, anchor_ref, dir_ref, app_ref, grad_ref, out_ref, tile_ref):
    row = lax.broadcasted_iota(jnp.int32, out_ref.shape, 1)
    out_ref[...] = jnp.where((row >= 10) & (row < 13), -1.0, 0.0)
    for t in range(tiles):
        lanes = pl.ds(t * TILE, TILE)
        tile_ref[t] = jnp.zeros((ROWS, TILE), F32)
        tile_ref[t, 0:3, :] = anchor_ref[:, lanes]
        tile_ref[t, 3:6, :] = dir_ref[:, lanes]
        tile_ref[t, 6:7, :] = app_ref[t : t + 1, :].astype(F32)
        tile_ref[t, 7:10, :] = grad_ref[:, lanes]
        for k in range(3):
            tile_ref[t, 10 + k : 11 + k, :] = jnp.full((1, TILE), ids_ref[t, k], jnp.int32).astype(F32)
        for k in range(3):
            out_ref[ids_ref[t, k]] = tile_ref[t]


def weight_kernel(
    pos_ref, tw_ref, density_ref, feature_ref, view_ref, cw_ref, rad_ref, table_ref,
    wp, wfd, wvc, wr, stack, w0t, w1t, wfdt, wct, wrt, pad, narrow,
):
    pad[...] = jnp.zeros_like(pad)
    pad[0 : pos_ref.shape[0], :] = pos_ref[...].astype(F32)
    wp[...] = pad[...].T.astype(BF16)
    narrow[...] = jnp.zeros_like(narrow)
    narrow[0 : cw_ref.shape[0], :] = cw_ref[...].astype(F32)
    narrow[cw_ref.shape[0] : cw_ref.shape[0] + view_ref.shape[0], :] = view_ref[...].astype(F32)
    wvc[...] = narrow[...].T.astype(BF16)
    wct[...] = cw_ref[...]
    wfd[0:128, :] = feature_ref[...]
    pad[0:16, :] = jnp.zeros((16, pad.shape[1]), F32)
    pad[DENSE - 128 : DENSE - 127, :] = density_ref[...].astype(F32)
    wfd[128:EDGE, :] = pad[0 : EDGE - 128, :].astype(BF16)
    narrow[0:16, :] = jnp.zeros((16, narrow.shape[1]), F32)
    narrow[0 : rad_ref.shape[0], :] = rad_ref[...].astype(F32)
    wr[...] = narrow[0:16, :].astype(BF16)
    wrt[...] = wr[...].T
    wfdt[...] = wfd[...].T
    w0t[...] = tw_ref[0].T
    w1t[...] = tw_ref[1].T
    codes = table_ref.shape[0]
    for hi in range(table_ref.shape[1] // LOW):
        stack[hi * codes : (hi + 1) * codes, :] = table_ref[:, hi * LOW : (hi + 1) * LOW]


def composite(density, radiance):
    decay = [jnp.exp(-d * spacing) for d in density]
    passed, run = [], jnp.zeros_like(density[0])
    for d in density:
        passed.append(jnp.exp(-run))
        run = run + d * spacing
    weight = [p * (1.0 - e) for p, e in zip(passed, decay)]
    color = [sum(w * r for w, r in zip(weight, radiance[c])) for c in range(3)]
    return decay, passed, weight, color, sum(weight)


def distance(rays, centers):
    total = 1.0
    for c in range(3):
        offset = rays[:, c, :] - centers[0, c]
        total = total + offset * offset
    return total


def forward_kernel(
    group, codes, rays_ref, center_ref, wp, tw, wfd, wvc, wr, stack,
    partial_ref, code_ref, h0_ref, h1_ref, h2_ref, shade_ref, vc_ref, density_ref, radiance_ref,
    dl_scr, rl_scr,
):
    step = pl.program_id(0)
    highs = stack.shape[0] // codes
    for j in range(group):
        tile = step * group + j
        at = slice(j * COLS, (j + 1) * COLS)
        rays = rays_ref[tile]
        points = []
        for c in range(3):
            base = rays[c : c + 1, :]
            move = rays[3 + c : 4 + c, :]
            points.append(
                jnp.concatenate(
                    [base + ((s + 0.5) * spacing) * move - center_ref[0, c] for s in range(SAMPLES)], 1
                )
            )
        code = encode(points, FREQ, wp.shape[1]).astype(BF16)
        code_ref[:, at] = code
        h0 = softplus(dot(wp[...], code)).astype(BF16)
        h0_ref[:, at] = h0
        h1 = softplus(dot(tw[0], h0)).astype(BF16)
        h1_ref[:, at] = h1
        h2 = softplus(dot(tw[1], h1)).astype(BF16)
        h2_ref[:, at] = h2
        feature = dot(wfd[...], h2)
        dl_scr[pl.ds(tile, 1), :] = feature[DENSE : DENSE + 1, :]
        view = encode([rays[3 + c : 4 + c, :] for c in range(3)], VFREQ, VCODE)
        ids = rays[6:7, :].astype(jnp.int32)
        low, high = ids & (LOW - 1), ids // LOW
        hit = (lax.broadcasted_iota(jnp.int32, (LOW, TILE), 0) == low).astype(F32).astype(BF16)
        picked = dot(stack[...], hit)
        app = jnp.zeros((codes, TILE), F32)
        for hi in range(highs):
            app = app + jnp.where(high == hi, picked[hi * codes : (hi + 1) * codes], 0.0)
        vc = jnp.concatenate([app, view], 0).astype(BF16)
        vc_ref[:, j * TILE : (j + 1) * TILE] = vc
        per_ray = dot(wvc[...], vc)
        shaded = softplus(feature[0:128] + jnp.concatenate([per_ray] * SAMPLES, 1)).astype(BF16)
        shade_ref[:, at] = shaded
        logits = dot(wr[...], shaded)
        for c in range(3):
            rl_scr[c, pl.ds(tile, 1), :] = logits[c : c + 1, :]

    @pl.when(step == pl.num_programs(0) - 1)
    def _():
        logit = dl_scr[...]
        density = jnp.maximum(logit, 0.0) + jnp.log1p(jnp.exp(-jnp.abs(logit)))
        density_ref[0] = density
        density_ref[1] = 1.0 / (1.0 + jnp.exp(-logit))
        radiance = [1.0 / (1.0 + jnp.exp(-rl_scr[c])) for c in range(3)]
        for c in range(3):
            radiance_ref[c] = radiance[c]
        lanes = [slice(s * TILE, (s + 1) * TILE) for s in range(SAMPLES)]
        _, _, _, color, opacity = composite(
            [density[:, at] for at in lanes], [[radiance[c][:, at] for at in lanes] for c in range(3)]
        )
        share = (0.1 + opacity) / distance(rays_ref, center_ref)
        for c in range(3):
            partial_ref[c] = share * color[c]
        partial_ref[3] = share


def cotangents(rays_ref, center_ref, parts_ref, density_ref, radiance_ref, cot_scr):
    ids = [rays_ref[:, 10 + k, :] for k in range(3)]
    live = ids[0] >= 0.0
    summed = [jnp.zeros_like(ids[0]) for _ in range(4)]
    for b in range(parts_ref.shape[0]):
        mine = (ids[0] == b) | (ids[1] == b) | (ids[2] == b)
        for c in range(4):
            summed[c] = summed[c] + jnp.where(mine, parts_ref[b, c], 0.0)
    norm = 1.0 / jnp.where(live, summed[3], 1.0)
    got = [jnp.where(live, rays_ref[:, 7 + c, :] * loss_scale, 0.0) * norm for c in range(3)]
    got_share = -sum(got[c] * summed[c] for c in range(3)) * norm
    lanes = [slice(s * TILE, (s + 1) * TILE) for s in range(SAMPLES)]
    density = [density_ref[0, :, at] for at in lanes]
    gate = [density_ref[1, :, at] for at in lanes]
    radiance = [[radiance_ref[c, :, at] for at in lanes] for c in range(3)]
    decay, passed, weight, color, opacity = composite(density, radiance)
    far = 1.0 / distance(rays_ref, center_ref)
    share = (0.1 + opacity) * far
    d_color = [got[c] * share for c in range(3)]
    d_opacity = (sum(got[c] * color[c] for c in range(3)) + got_share) * far
    d_weight = [
        sum(d_color[c] * radiance[c][s] for c in range(3)) + d_opacity for s in range(SAMPLES)
    ]
    later = jnp.zeros_like(far)
    cot_scr[...] = jnp.zeros_like(cot_scr)
    for s in reversed(range(SAMPLES)):
        d_optical = passed[s] * decay[s] * d_weight[s] - later
        later = later + weight[s] * d_weight[s]
        cot_scr[:, 3, lanes[s]] = d_optical * spacing * gate[s]
        for c in range(3):
            r = radiance[c][s]
            cot_scr[:, c, lanes[s]] = d_color[c] * weight[s] * r * (1.0 - r)


def color_kernel(
    group, tiles, ids_ref, me_ref, rays_ref, center_ref, parts_ref, density_ref, radiance_ref,
    h2_ref, shade_ref, vc_ref, wfdt, wct, wrt, low_ref,
    colors_ref, keep_ref, send_ref, column_ref, d2_ref,
    cot_scr, head_ref, fd_scr, r_scr, vc_scr,
):
    step = pl.program_id(0)

    @pl.when(step == 0)
    def _():
        cotangents(rays_ref, center_ref, parts_ref, density_ref, radiance_ref, cot_scr)
        me = me_ref[0]
        for t in range(tiles):
            summed = [
                sum(parts_ref[ids_ref[t, k], c, pl.ds(me, 1), :] for k in range(3)) for c in range(4)
            ]
            for c in range(3):
                colors_ref[c : c + 1, t * TILE : (t + 1) * TILE] = summed[c] / summed[3]
        for ref in (fd_scr, r_scr, vc_scr):
            ref[...] = jnp.zeros_like(ref)

    for j in range(group):
        tile = step * group + j
        at = slice(j * COLS, (j + 1) * COLS)
        cot = cot_scr[tile]
        low = jnp.concatenate([cot, jnp.zeros_like(cot)], 0).astype(BF16)
        shaded = shade_ref[:, at]
        d_feature = dot(wrt[...], low) * slope(shaded)
        r_scr[...] += dot_nt(low, shaded)
        d_ray = (
            d_feature[:, 0:TILE]
            + d_feature[:, TILE : 2 * TILE]
            + d_feature[:, 2 * TILE : 3 * TILE]
            + d_feature[:, 3 * TILE :]
        ).astype(BF16)
        vc = vc_ref[:, j * TILE : (j + 1) * TILE]
        vc_scr[...] += dot_nt(vc, d_ray)
        lanes = slice(j * TILE, (j + 1) * TILE)
        codes = wct.shape[0]
        column_ref[0:codes, lanes] = dot(wct[...], d_ray).astype(BF16).astype(F32)
        column_ref[codes:, lanes] = jnp.broadcast_to(
            rays_ref[tile, 6:7, :], (column_ref.shape[0] - codes, TILE)
        )
        h2 = h2_ref[:, at]
        edge = jnp.concatenate([d_feature.astype(BF16), low], 0)
        fd_scr[...] += dot_nt(edge, h2)
        d2_ref[:, at] = (dot(wfdt[...], edge) * slope(h2)).astype(BF16)

    @pl.when(step == pl.num_programs(0) - 1)
    def _():
        head_ref[0:EDGE, :] = fd_scr[...]
        head_ref[EDGE - 8 : EDGE, 0:128] = r_scr[0:8, :]
        half = vc_scr.shape[0] // 2
        head_ref[EDGE : EDGE + half, 0:128] = vc_scr[0:half, :]
        head_ref[EDGE : EDGE + half, 128:256] = vc_scr[half:, :]
        h = keep_ref.shape[0]
        halves(low_ref, head_ref[0:h, :], head_ref[h : 2 * h, :], keep_ref, send_ref)


def halves(low_ref, first, second, keep_ref, send_ref):
    low = low_ref[0] == 1
    keep_ref[...] = jnp.where(low, first, second)
    send_ref[...] = jnp.where(low, second, first)


def trunk_kernel(
    group, low_ref, d2_ref, h1_ref, h0_ref, code_ref, w1t, w0t,
    keep1, send1, keep0, send0, grad,
):
    step = pl.program_id(0)
    hid = w1t.shape[0]

    @pl.when(step == 0)
    def _():
        grad[...] = jnp.zeros_like(grad)

    for j in range(group):
        at = slice(j * COLS, (j + 1) * COLS)
        d2, h1 = d2_ref[:, at], h1_ref[:, at]
        grad[0:hid, :] += dot_nt(d2, h1)
        d1 = (dot(w1t[...], d2) * slope(h1)).astype(BF16)
        h0 = h0_ref[:, at]
        grad[hid : 2 * hid, :] += dot_nt(d1, h0)
        d0 = (dot(w0t[...], d1) * slope(h0)).astype(BF16)
        grad[2 * hid :, :] += dot_nt(code_ref[:, at], d0)

    @pl.when(step == pl.num_programs(0) - 1)
    def _():
        h = keep1.shape[0]
        halves(low_ref, grad[0:h, :], grad[h : 2 * h, :], keep1, send1)
        halves(low_ref, grad[2 * h : 3 * h, :], grad[3 * h : 4 * h, :], keep0, send0)


def table_kernel(side_ref, own_ref, near_ref, far0_ref, far1_ref, out_ref, cols, lhs, total):
    side = side_ref[0]
    codes, rays = out_ref.shape[0], own_ref.shape[1]
    other = side + 1 - 2 * (side & 1)
    cols[side] = own_ref[...]
    cols[other] = near_ref[...]
    cols[3 - side] = far0_ref[...]
    cols[3 - other] = far1_ref[...]
    highs = out_ref.shape[1] // LOW
    chunk = lhs.shape[1]
    total[...] = jnp.zeros_like(total)
    for z in range(4):
        for start in range(0, rays, chunk):
            ids = cols[z, codes : codes + 1, start : start + chunk].astype(jnp.int32)
            low, high = ids & (LOW - 1), ids // LOW
            value = cols[z, 0:codes, start : start + chunk].astype(BF16)
            for hi in range(highs):
                lhs[hi * codes : (hi + 1) * codes, :] = jnp.where(high == hi, value, jnp.zeros_like(value))
            hit = (lax.broadcasted_iota(jnp.int32, (LOW, chunk), 0) == low).astype(F32).astype(BF16)
            total[...] += dot_nt(lhs[...], hit)
    for hi in range(highs):
        out_ref[:, hi * LOW : (hi + 1) * LOW] = total[hi * codes : (hi + 1) * codes]


def join(low_ref, mine, other, out_ref):
    low = low_ref[0] == 1
    h = mine.shape[0]
    out_ref[0:h, :] = jnp.where(low, mine[...], other[...])
    out_ref[h : 2 * h, :] = jnp.where(low, other[...], mine[...])


def head_kernel(low_ref, mine, other, density_ref, feature_ref, view_ref, code_ref, rad_ref, head):
    join(low_ref, mine, other, head)
    feature_ref[...] = head[0:128, :]
    density_ref[...] = head[DENSE : DENSE + 1, :]
    for c in range(3):
        rad_ref[c] = head[EDGE - 8 + c : EDGE - 7 + c, 0:128]
    code_ref[...] = head[EDGE : EDGE + VCODE, 0:128]
    for c in range(view_ref.shape[0]):
        view_ref[c] = head[EDGE + c : EDGE + c + 1, 128:256]


def sides_kernel(low_ref, mine1, other1, mine0, other0, trunk_ref, pos_ref, grad):
    h = 2 * mine1.shape[0]
    join(low_ref, mine1, other1, grad.at[0:h])
    join(low_ref, mine0, other0, grad.at[h : 2 * h])
    hid = trunk_ref.shape[1]
    trunk_ref[1] = grad[0:hid, :]
    trunk_ref[0] = grad[hid : 2 * hid, :]
    for c in range(pos_ref.shape[0]):
        pos_ref[c] = grad[2 * hid + c : 2 * hid + c + 1, :]


def shape_of(*dims, dtype=F32):
    return jax.ShapeDtypeStruct(dims, dtype)


def local(
    anchors,
    directions,
    app_ids,
    block_ids,
    color_grad,
    block_centers,
    pos_weight,
    trunk_weight,
    density_weight,
    feature_weight,
    view_weight,
    code_weight,
    radiance_weight,
    code_table,
):
    tiles = block_ids.shape[0]
    blocks = lax.axis_size("blk")
    reps = lax.axis_size("rep")
    assert reps == 4
    group = 2 if blocks % 2 == 0 else 1
    hid = pos_weight.shape[1]
    codes, entries = code_table.shape[1:]
    params = pltpu.CompilerParams(vmem_limit_bytes=58 * 1024 * 1024)

    send = pl.pallas_call(
        functools.partial(send_kernel, tiles),
        out_shape=shape_of(blocks, ROWS, TILE),
        in_specs=[smem()] + [vmem()] * 4,
        out_specs=vmem(),
        scratch_shapes=[pltpu.VMEM((tiles, ROWS, TILE), F32)],
        name="send",
    )(block_ids, anchors, directions, app_ids.reshape(tiles, TILE), color_grad)
    rays = lax.all_to_all(send, "blk", split_axis=0, concat_axis=0, tiled=True)

    trunk = trunk_weight[0]
    positions, views = pos_weight.shape[2], view_weight.shape[2]
    wp, wfd, wvc, wr, stack, w0t, w1t, wfdt, wct, wrt = pl.pallas_call(
        weight_kernel,
        out_shape=tuple(
            shape_of(*dims, dtype=BF16)
            for dims in (
                (hid, 64), (EDGE, hid), (128, 64), (16, 128), (entries // LOW * codes, LOW),
                (hid, hid), (hid, hid), (hid, EDGE), (codes, 128), (128, 16),
            )
        ),
        in_specs=[vmem()] * 8,
        out_specs=(vmem(),) * 10,
        scratch_shapes=[pltpu.VMEM((64, hid), F32), pltpu.VMEM((64, 128), F32)],
        name="weights",
    )(
        pos_weight[0].T, trunk, density_weight, feature_weight[0], view_weight[0].T,
        code_weight[0].T, radiance_weight[0], code_table[0],
    )

    centers = block_centers.T
    n = blocks * COLS
    steps = blocks // group
    wide = lambda rows, cols: pl.BlockSpec((rows, group * cols), lambda i: (0, i))
    saved_shapes = (
        shape_of(64, n, dtype=BF16),
        shape_of(hid, n, dtype=BF16),
        shape_of(hid, n, dtype=BF16),
        shape_of(hid, n, dtype=BF16),
        shape_of(128, n, dtype=BF16),
        shape_of(64, blocks * TILE, dtype=BF16),
        shape_of(2, blocks, COLS),
        shape_of(3, blocks, COLS),
    )
    saved_specs = (
        wide(64, COLS),
        wide(hid, COLS),
        wide(hid, COLS),
        wide(hid, COLS),
        wide(128, COLS),
        wide(64, TILE),
        whole((2, blocks, COLS)),
        whole((3, blocks, COLS)),
    )
    outs = pl.pallas_call(
        functools.partial(forward_kernel, group, codes),
        grid=(steps,),
        out_shape=(shape_of(4, blocks, TILE),) + saved_shapes,
        in_specs=[
            whole(rays.shape),
            smem(),
            whole(wp.shape),
            whole(trunk.shape),
            whole(wfd.shape),
            whole(wvc.shape),
            whole(wr.shape),
            whole(stack.shape),
        ],
        out_specs=(whole((4, blocks, TILE)),) + saved_specs,
        scratch_shapes=[pltpu.VMEM((blocks, COLS), F32), pltpu.VMEM((3, blocks, COLS), F32)],
        compiler_params=params,
        name="forward",
    )(rays, centers, wp, trunk, wfd, wvc, wr, stack)
    partial, saved = outs[0], outs[1:]
    code, h0, h1, h2, shaded, vc, density, radiance = saved
    parts = lax.all_gather(partial, "blk", axis=0, tiled=False)

    me = lax.axis_index("blk").astype(jnp.int32)[None]
    side = lax.axis_index("rep").astype(jnp.int32)[None]
    head_rows, trunk_rows = EDGE + VCODE, 2 * hid + 64
    code_rows = codes + 8
    half = lambda rows, parts: shape_of(rows // (2 * parts), hid)
    low = ((side == 0) | (side == 3)).astype(jnp.int32)
    square = lambda k, m: pl.CostEstimate(flops=2 * k * m * n, bytes_accessed=2 * k * n, transcendentals=k * n)
    colors, keep, send, columns, d2 = pl.pallas_call(
        functools.partial(color_kernel, group, tiles),
        grid=(steps,),
        out_shape=(
            shape_of(3, tiles * TILE),
            half(head_rows, 1),
            half(head_rows, 1),
            shape_of(code_rows, blocks * TILE),
            shape_of(hid, n, dtype=BF16),
        ),
        in_specs=[smem(), smem(), whole(rays.shape), smem(), whole(parts.shape)]
        + [saved_specs[6], saved_specs[7]]
        + list(saved_specs[3:6])
        + [whole(w.shape) for w in (wfdt, wct, wrt)]
        + [smem()],
        out_specs=(
            whole((3, tiles * TILE)),
            whole((head_rows // 2, hid)),
            whole((head_rows // 2, hid)),
            wide(code_rows, TILE),
            wide(hid, COLS),
        ),
        scratch_shapes=[
            pltpu.VMEM((blocks, 8, COLS), F32),
            pltpu.VMEM((head_rows, hid), F32),
            pltpu.VMEM((EDGE, hid), F32),
            pltpu.VMEM((16, 128), F32),
            pltpu.VMEM((64, 128), F32),
        ],
        compiler_params=params,
        cost_estimate=square(hid, 4 * EDGE),
        name="color",
    )(block_ids, me, rays, centers, parts, density, radiance, h2, shaded, vc, wfdt, wct, wrt, low)

    part = half(trunk_rows, 2)
    trunk_call = pl.pallas_call(
        functools.partial(trunk_kernel, group),
        grid=(steps,),
        out_shape=(part,) * 4,
        in_specs=[smem()] + [wide(x, COLS) for x in (hid, hid, hid, 64)] + [whole((hid, hid))] * 2,
        out_specs=(whole(part.shape),) * 4,
        scratch_shapes=[pltpu.VMEM((trunk_rows, hid), F32)],
        compiler_params=params,
        cost_estimate=square(hid, 8 * hid),
        name="trunk",
    )
    keep1, send1, keep0, send0 = trunk_call(low, d2, h1, h0, code, w1t, w0t)

    swap = lambda x: lax.ppermute(x, "rep", [(0, 1), (1, 0), (2, 3), (3, 2)])
    mirror = lambda x: lax.ppermute(x, "rep", [(0, 3), (3, 0), (1, 2), (2, 1)])
    near = swap(columns)
    far0 = mirror(columns)
    far1 = mirror(near)

    def rep_sum(keep, send):
        got = swap(send)
        pair = keep + got
        got = mirror(pair)
        mine = pair + got
        return mine, swap(mine)

    head_sum = rep_sum(keep, send)
    sums = rep_sum(keep1, send1) + rep_sum(keep0, send0)
    rays_n = blocks * TILE
    chunk = min(rays_n, 1024)
    table_call = pl.pallas_call(
        table_kernel,
        out_shape=shape_of(codes, entries),
        in_specs=[smem()] + [vmem()] * 4,
        out_specs=vmem(),
        scratch_shapes=[
            pltpu.VMEM((reps, code_rows, rays_n), F32),
            pltpu.VMEM((entries // LOW * codes, chunk), BF16),
            pltpu.VMEM((entries // LOW * codes, LOW), F32),
        ],
        compiler_params=params,
        name="table",
    )
    table_grad = table_call(side, columns, near, far0, far1)

    heads_call = pl.pallas_call(
        head_kernel,
        out_shape=(
            shape_of(1, hid),
            shape_of(128, hid),
            shape_of(views, 1, 128),
            shape_of(codes, 128),
            shape_of(3, 1, 128),
        ),
        in_specs=[smem()] + [vmem()] * 2,
        out_specs=(vmem(),) * 5,
        scratch_shapes=[pltpu.VMEM((head_rows, hid), F32)],
        name="heads",
    )
    grad_density, grad_feature, grad_view, grad_code, grad_rad = heads_call(low, *head_sum)
    grad_trunk, grad_pos = pl.pallas_call(
        sides_kernel,
        out_shape=(shape_of(2, hid, hid), shape_of(positions, 1, hid)),
        in_specs=[smem()] + [vmem()] * 4,
        out_specs=(vmem(),) * 2,
        scratch_shapes=[pltpu.VMEM((trunk_rows, hid), F32)],
        name="sides",
    )(low, *sums)
    return (
        colors,
        jnp.transpose(grad_pos, (1, 2, 0)),
        grad_trunk[None],
        grad_density,
        grad_feature[None],
        jnp.transpose(grad_view, (1, 2, 0)),
        grad_code.T[None],
        jnp.transpose(grad_rad, (1, 0, 2)),
        table_grad[None],
    )


def solution(mesh):
    return jax.shard_map(
        local,
        mesh=mesh,
        in_specs=(
            P(None, ("blk", "rep")),
            P(None, ("blk", "rep")),
            P(("blk", "rep")),
            P(("blk", "rep"), None),
            P(None, ("blk", "rep")),
            P(None, "blk"),
            P("blk", None, None),
            P("blk", None, None, None),
            P("blk", None),
            P("blk", None, None),
            P("blk", None, None),
            P("blk", None, None),
            P("blk", None, None),
            P("blk", None, None),
        ),
        out_specs=(
            P(None, ("blk", "rep")),
            P("blk", None, None),
            P("blk", None, None, None),
            P("blk", None),
            P("blk", None, None),
            P("blk", None, None),
            P("blk", None, None),
            P("blk", None, None),
            P("blk", None, None),
        ),
        check_vma=False,
    )
```

profile of v0, /device:TPU:0, one launch (start us, length us, event | category | flops | bytes accessed | tf_op | source)
XLA Modules:
  0.0 109.5 jit_solution(15586542081595984802)
XLA Ops:
  0.6 1.5 %send.1 = f32[8,16,128]{2,1,0:T(8,128)} custom-call(s32[2,3]{1,0:T(2,128)} %ids_ref.3, f32[3,256]{1,0:T(4,128)} %anchor_ref.1, f32[3,256]{1,0:T(4,128)} %dir_ref.1, s32[2,128]{1,0:T(2,128)} %bitcast.36, f32[3,256]{1,0:T(4,128)} %grad_ref.1), custom_call_target="tpu_custom_call" | custom-call | tf_op jit(solution)/shard_map/send/pallas_call | solution.py:427
  2.1 5.2 %all-to-all-start = ((f32[8,16,128]{2,1,0:T(8,128)}), f32[8,16,128]{2,1,0:T(8,128)S(1)}, u32[]{:S(2)}, u32[]{:S(2)}) async-start(f32[8,16,128]{2,1,0:T(8,128)} %send.1), calls=%async_computation | async-start | bytes 131072 | tf_op jit(solution)/shard_map/all_to_all | solution.py:435
  7.3 2.3 %weights.1 = (bf16[256,64]{1,0:T(8,128)(2,1)}, bf16[144,256]{1,0:T(8,128)(2,1)}, bf16[128,64]{1,0:T(8,128)(2,1)}, bf16[16,128]{1,0:T(8,128)(2,1)}, bf16[1024,256...) custom-call(bf16[63,256]{1,0:T(8,128)(2,1)} %bitcast.33, ...), custom_call_target="tpu_custom_call" | custom-call | tf_op jit(solution)/shard_map/weights/pallas_call | solution.py:439
  9.6 2.7 %all-to-all-done.rays_ref = f32[8,16,128]{2,1,0:T(8,128)S(1)} async-done(((f32[8,16,128]{2,1,0:T(8,128)}), f32[8,16,128]{2,1,0:T(8,128)S(1)}, u32[]{:S(2)}, u32[]{:S(2)}) %all-to-all-start) | async-done | bytes 65568 | tf_op jit(solution)/shard_map/all_to_all | solution.py:435
  13.0 16.0 %forward.1 = (f32[4,8,128]{2,1,0:T(8,128)}, bf16[64,4096]{1,0:T(8,128)(2,1)}, bf16[256,4096]{1,0:T(8,128)(2,1)}, bf16[256,4096]{1,0:T(8,128)(2,1)}, bf16[256,409...) custom-call(f32[8,16,128]{2,1,0:T(8,128)} %copy-done.3, ...), custom_call_target="tpu_custom_call" | custom-call | tf_op jit(solution)/shard_map/forward/pallas_call | solution.py:481
  29.0 10.0 %all-gather = f32[32,8,128]{2,1,0:T(8,128)} all-gather(f32[4,8,128]{2,1,0:T(8,128)} %get-tuple-element.49), channel_id=2, replica_groups=mesh['blk'=8,'rep'=4] {'blk'}, dimensions={0}, use_global_device_ids=true | all-gather | bytes 147456 | tf_op jit(solution)/shard_map/all_gather | solution.py:502
  38.9 6.6 %color.1 = (f32[3,256]{1,0:T(4,128)}, f32[88,256]{1,0:T(8,128)}, f32[88,256]{1,0:T(8,128)}, f32[40,1024]{1,0:T(8,128)}, bf16[256,4096]{1,0:T(8,128)(2,1)}) custom-call(s32[2,3]{1,0:T(2,128)} %ids_ref.3, s32[1]{0:T(128)} %bitcast.me_ref, f32[8,16,128]{2,1,0:T(8,128)} %copy-done.3, f32[1,3]{1,0:T(1,128)} %bitcast.39, f32[8,4,8,128]{3,2,1,0:T(8,128)} %bitcast.31, ...), custom_call_target="tpu_custom_call" | custom-call | flops 1207959552 | bytes 2097152 | tf_op jit(solution)/shard_map/color/pallas_call | solution.py:511
  45.5 7.4 %trunk.1 = (f32[144,256]{1,0:T(8,128)}, f32[144,256]{1,0:T(8,128)}, f32[144,256]{1,0:T(8,128)}, f32[144,256]{1,0:T(8,128)}) custom-call(s32[1]{0:T(128)S(6)} %convert_element_type.3.low_ref, bf16[256,4096]{1,0:T(8,128)(2,1)} %get-tuple-element.59.d2_ref, bf16[256,4096]{1,0:T(8,128)(2,1)} %get-tuple-element.60.h1_ref, ...), custom_call_target="tpu_custom_call" | custom-call | flops 4294967296 | bytes 2097152 | tf_op jit(solution)/shard_map/trunk/pallas_call | solution.py:557
  52.9 1.6 %collective-permute-start = (f32[144,256]{1,0:T(8,128)}, f32[144,256]{1,0:T(8,128)S(1)}, u32[]{:S(2)}, u32[]{:S(2)}) collective-permute-start(f32[144,256]{1,0:T(8,128)} %get-tuple-element.66), channel_id=1, source_target_pairs={{0,1},{1,0},{2,3},{3,2},{4,5},{5,4},{6,7},{7,6},{8,9},{9,8},{10,11... | collective-permute-start | bytes 442376 | tf_op jit(solution)/shard_map/ppermute | solution.py:559
  55.0 1.6 %collective-permute-start.9 = (f32[40,1024]{1,0:T(8,128)S(1)}, f32[40,1024]{1,0:T(8,128)S(1)}, u32[]{:S(2)}, u32[]{:S(2)}) collective-permute-start(f32[40,1024]{1,0:T(8,128)S(1)} %copy-done.4), channel_id=1, source_target_pairs={{0,1},{1,0},{2,3},{3,2},{4,5},{5,4},{6,7},{7,6},{8,9},{9,8},{10,11... | collective-permute-start | bytes 491528 | tf_op jit(solution)/shard_map/ppermute | solution.py:559
  56.5 3.3 %collective-permute-done = f32[144,256]{1,0:T(8,128)S(1)} collective-permute-done((f32[144,256]{1,0:T(8,128)}, f32[144,256]{1,0:T(8,128)S(1)}, u32[]{:S(2)}, u32[]{:S(2)}) %collective-permute-start) | collective-permute-done | bytes 147488 | tf_op jit(solution)/shard_map/ppermute | solution.py:559
  60.8 3.7 %collective-permute-start.1 = (f32[144,256]{1,0:T(8,128)S(1)}, f32[144,256]{1,0:T(8,128)S(1)}, u32[]{:S(2)}, u32[]{:S(2)}) collective-permute-start(f32[144,256]{1,0:T(8,128)S(1)} %add.18), channel_id=1, source_target_pairs={{0,3},{3,0},{1,2},{2,1},{4,7},{7,4},{5,6},{6,5},{8,11},{11,8},{9,1... | collective-permute-start | bytes 442376 | tf_op jit(solution)/shard_map/ppermute | solution.py:560
  64.5 0.9 add.20
  65.4 2.2 %collective-permute-start.4 = (f32[144,256]{1,0:T(8,128)S(1)}, f32[144,256]{1,0:T(8,128)S(1)}, u32[]{:S(2)}, u32[]{:S(2)}) collective-permute-start(f32[144,256]{1,0:T(8,128)S(1)} %add.20), channel_id=1, source_target_pairs={{0,3},{3,0},{1,2},{2,1},{4,7},{7,4},{5,6},{6,5},{8,11},{11,8},{9,1... | collective-permute-start | bytes 442376 | tf_op jit(solution)/shard_map/ppermute | solution.py:560
  67.6 8.7 %collective-permute-done.6 = f32[88,256]{1,0:T(8,128)S(1)} collective-permute-done((f32[88,256]{1,0:T(8,128)S(1)}, f32[88,256]{1,0:T(8,128)S(1)}, u32[]{:S(2)}, u32[]{:S(2)}) %collective-permute-start.6) | collective-permute-done | bytes 90144 | tf_op jit(solution)/shard_map/ppermute | solution.py:559
  76.3 1.5 %collective-permute-start.7 = (f32[88,256]{1,0:T(8,128)S(1)}, f32[88,256]{1,0:T(8,128)S(1)}, u32[]{:S(2)}, u32[]{:S(2)}) collective-permute-start(f32[88,256]{1,0:T(8,128)S(1)} %add.22), channel_id=1, source_target_pairs={{0,3},{3,0},{1,2},{2,1},{4,7},{7,4},{5,6},{6,5},{8,11},{11,8},{9,1... | collective-permute-start | bytes 270344 | tf_op jit(solution)/shard_map/ppermute | solution.py:560
  77.8 2.3 %collective-permute-start.10 = (f32[40,1024]{1,0:T(8,128)S(1)}, f32[40,1024]{1,0:T(8,128)S(1)}, u32[]{:S(2)}, u32[]{:S(2)}) collective-permute-start(f32[40,1024]{1,0:T(8,128)S(1)} %copy-done.4), channel_id=1, source_target_pairs={{0,3},{3,0},{1,2},{2,1},{4,7},{7,4},{5,6},{6,5},{8,11},{11,8},{9,1... | collective-permute-start | bytes 491528 | tf_op jit(solution)/shard_map/ppermute | solution.py:560
  80.2 1.5 %collective-permute-start.11 = (f32[40,1024]{1,0:T(8,128)S(1)}, f32[40,1024]{1,0:T(8,128)S(1)}, u32[]{:S(2)}, u32[]{:S(2)}) collective-permute-start(f32[40,1024]{1,0:T(8,128)S(1)} %collective-permute-done.9.near_ref), channel_id=1, source_target_pairs={{0,3},{3,0},{1,2},{2,1},{4,7},{7,4},{5,6},{6,5},{8,11},{11,8},{9,1... | collective-permute-start | bytes 491528 | tf_op jit(solution)/shard_map/ppermute | solution.py:560
  81.8 2.1 %collective-permute-start.5 = (f32[144,256]{1,0:T(8,128)S(1)}, f32[144,256]{1,0:T(8,128)S(1)}, u32[]{:S(2)}, u32[]{:S(2)}) collective-permute-start(f32[144,256]{1,0:T(8,128)S(1)} %add.21.mine0), channel_id=1, source_target_pairs={{0,1},{1,0},{2,3},{3,2},{4,5},{5,4},{6,7},{7,6},{8,9},{9,8},{10,11... | collective-permute-start | bytes 442376 | tf_op jit(solution)/shard_map/ppermute | solution.py:559
  83.9 4.8 %collective-permute-start.8 = (f32[88,256]{1,0:T(8,128)S(1)}, f32[88,256]{1,0:T(8,128)S(1)}, u32[]{:S(2)}, u32[]{:S(2)}) collective-permute-start(f32[88,256]{1,0:T(8,128)S(1)} %add.23.mine), channel_id=1, source_target_pairs={{0,1},{1,0},{2,3},{3,2},{4,5},{5,4},{6,7},{7,6},{8,9},{9,8},{10,11... | collective-permute-start | bytes 270344 | tf_op jit(solution)/shard_map/ppermute | solution.py:559
  88.7 9.4 %collective-permute-done.8.other = f32[88,256]{1,0:T(8,128)S(1)} collective-permute-done((f32[88,256]{1,0:T(8,128)S(1)}, f32[88,256]{1,0:T(8,128)S(1)}, u32[]{:S(2)}, u32[]{:S(2)}) %collective-permute-start.8) | collective-permute-done | bytes 90144 | tf_op jit(solution)/shard_map/ppermute | solution.py:559
  98.7 1.6 %heads.1 = (f32[1,256]{1,0:T(1,128)}, f32[128,256]{1,0:T(8,128)}, f32[27,1,128]{2,1,0:T(1,128)}, f32[32,128]{1,0:T(8,128)}, f32[3,1,128]{2,1,0:T(1,128)}) custom-call(s32[1]{0:T(128)S(6)} %convert_element_type.3.low_ref, f32[88,256]{1,0:T(8,128)} %copy-done.2, f32[88,256]{1,0:T(8,128)} %copy-done.11), custom_call_target="tpu_custom_call" | custom-call | tf_op jit(solution)/shard_map/heads/pallas_call | solution.py:605
  101.7 4.5 %table.1 = f32[32,8192]{1,0:T(8,128)} custom-call(s32[1]{0:T(128)} %bitcast.14.side_ref, f32[40,1024]{1,0:T(8,128)} %get-tuple-element.78.own_ref, f32[40,1024]{1,0:T(8,128)} %copy-done.5, f32[40,1024]{1,0:T(8,128)} %copy-done.6, f32[40,1024]{1,0:T(8,128)} %copy-done.7), custom_call_target="tpu_custom_call" | custom-call | tf_op jit(solution)/shard_map/table/pallas_call | solution.py:589
  107.5 2.0 %sides.1 = (f32[2,256,256]{2,1,0:T(8,128)}, f32[63,1,256]{2,1,0:T(1,128)}) custom-call(s32[1]{0:T(128)S(6)} %convert_element_type.3.low_ref, f32[144,256]{1,0:T(8,128)} %copy-done, f32[144,256]{1,0:T(8,128)} %copy-done.8, f32[144,256]{1,0:T(8,128)} %copy-done.1, f32[144,256]{1,0:T(8,128)} %copy-done.9), custom_call_target="tpu_custom_call" | custom-call | tf_op jit(solution)/shard_map/sides/pallas_call | solution.py:606
  (43 shorter events, 5.4 us)
Async XLA Ops:
  2.1 10.2 %all-to-all-start = ((f32[8,16,128]{2,1,0:T(8,128)}), f32[8,16,128]{2,1,0:T(8,128)S(1)}, u32[]{:S(2)}, u32[]{:S(2)}) async-start(f32[8,16,128]{2,1,0:T(8,128)} %send.1), calls=%async_computation | async-start | bytes 131072 | tf_op jit(solution)/shard_map/all_to_all | solution.py:435
  45.5 9.4 %copy-start.4 = (f32[40,1024]{1,0:T(8,128)S(1)}, f32[40,1024]{1,0:T(8,128)}, u32[]{:S(2)}) copy-start(f32[40,1024]{1,0:T(8,128)} %get-tuple-element.78.own_ref) | copy-start | bytes 491524
  45.5 22.1 %copy-start.12 = (f32[88,256]{1,0:T(8,128)S(1)}, f32[88,256]{1,0:T(8,128)}, u32[]{:S(2)}) copy-start(f32[88,256]{1,0:T(8,128)} %get-tuple-element.72) | copy-start | bytes 270340
  45.5 30.7 %copy-start.10 = (f32[88,256]{1,0:T(8,128)S(1)}, f32[88,256]{1,0:T(8,128)}, u32[]{:S(2)}) copy-start(f32[88,256]{1,0:T(8,128)} %get-tuple-element.71) | copy-start | bytes 270340
  52.9 6.9 %collective-permute-start = (f32[144,256]{1,0:T(8,128)}, f32[144,256]{1,0:T(8,128)S(1)}, u32[]{:S(2)}, u32[]{:S(2)}) collective-permute-start(f32[144,256]{1,0:T(8,128)} %get-tuple-element.66), channel_id=1, source_target_pairs={{0,1},{1,0},{2,3},{3,2},{4,5},{5,4},{6,7},{7,6},{8,9},{9,8},{10,11... | collective-permute-start | bytes 442376 | tf_op jit(solution)/shard_map/ppermute | solution.py:559
  54.5 10.0 %collective-permute-start.3 = (f32[144,256]{1,0:T(8,128)}, f32[144,256]{1,0:T(8,128)S(1)}, u32[]{:S(2)}, u32[]{:S(2)}) collective-permute-start(f32[144,256]{1,0:T(8,128)} %get-tuple-element.68), channel_id=1, source_target_pairs={{0,1},{1,0},{2,3},{3,2},{4,5},{5,4},{6,7},{7,6},{8,9},{9,8},{10,11... | collective-permute-start | bytes 442376 | tf_op jit(solution)/shard_map/ppermute | solution.py:559
  55.0 25.2 %collective-permute-start.9 = (f32[40,1024]{1,0:T(8,128)S(1)}, f32[40,1024]{1,0:T(8,128)S(1)}, u32[]{:S(2)}, u32[]{:S(2)}) collective-permute-start(f32[40,1024]{1,0:T(8,128)S(1)} %copy-done.4), channel_id=1, source_target_pairs={{0,1},{1,0},{2,3},{3,2},{4,5},{5,4},{6,7},{7,6},{8,9},{9,8},{10,11... | collective-permute-start | bytes 491528 | tf_op jit(solution)/shard_map/ppermute | solution.py:559
  60.8 20.9 %collective-permute-start.1 = (f32[144,256]{1,0:T(8,128)S(1)}, f32[144,256]{1,0:T(8,128)S(1)}, u32[]{:S(2)}, u32[]{:S(2)}) collective-permute-start(f32[144,256]{1,0:T(8,128)S(1)} %add.18), channel_id=1, source_target_pairs={{0,3},{3,0},{1,2},{2,1},{4,7},{7,4},{5,6},{6,5},{8,11},{11,8},{9,1... | collective-permute-start | bytes 442376 | tf_op jit(solution)/shard_map/ppermute | solution.py:560
  65.4 16.4 %collective-permute-start.4 = (f32[144,256]{1,0:T(8,128)S(1)}, f32[144,256]{1,0:T(8,128)S(1)}, u32[]{:S(2)}, u32[]{:S(2)}) collective-permute-start(f32[144,256]{1,0:T(8,128)S(1)} %add.20), channel_id=1, source_target_pairs={{0,3},{3,0},{1,2},{2,1},{4,7},{7,4},{5,6},{6,5},{8,11},{11,8},{9,1... | collective-permute-start | bytes 442376 | tf_op jit(solution)/shard_map/ppermute | solution.py:560
  67.6 8.7 %collective-permute-start.6 = (f32[88,256]{1,0:T(8,128)S(1)}, f32[88,256]{1,0:T(8,128)S(1)}, u32[]{:S(2)}, u32[]{:S(2)}) collective-permute-start(f32[88,256]{1,0:T(8,128)S(1)} %copy-done.12), channel_id=1, source_target_pairs={{0,1},{1,0},{2,3},{3,2},{4,5},{5,4},{6,7},{7,6},{8,9},{9,8},{10,11... | collective-permute-start | bytes 270344 | tf_op jit(solution)/shard_map/ppermute | solution.py:559
  76.3 7.6 %collective-permute-start.7 = (f32[88,256]{1,0:T(8,128)S(1)}, f32[88,256]{1,0:T(8,128)S(1)}, u32[]{:S(2)}, u32[]{:S(2)}) collective-permute-start(f32[88,256]{1,0:T(8,128)S(1)} %add.22), channel_id=1, source_target_pairs={{0,3},{3,0},{1,2},{2,1},{4,7},{7,4},{5,6},{6,5},{8,11},{11,8},{9,1... | collective-permute-start | bytes 270344 | tf_op jit(solution)/shard_map/ppermute | solution.py:560
  77.8 22.5 %collective-permute-start.10 = (f32[40,1024]{1,0:T(8,128)S(1)}, f32[40,1024]{1,0:T(8,128)S(1)}, u32[]{:S(2)}, u32[]{:S(2)}) collective-permute-start(f32[40,1024]{1,0:T(8,128)S(1)} %copy-done.4), channel_id=1, source_target_pairs={{0,3},{3,0},{1,2},{2,1},{4,7},{7,4},{5,6},{6,5},{8,11},{11,8},{9,1... | collective-permute-start | bytes 491528 | tf_op jit(solution)/shard_map/ppermute | solution.py:560
  80.2 20.1 %copy-start.5 = (f32[40,1024]{1,0:T(8,128)}, f32[40,1024]{1,0:T(8,128)S(1)}, u32[]{:S(2)}) copy-start(f32[40,1024]{1,0:T(8,128)S(1)} %collective-permute-done.9.near_ref) | copy-start | bytes 491524
  80.2 20.1 %collective-permute-start.11 = (f32[40,1024]{1,0:T(8,128)S(1)}, f32[40,1024]{1,0:T(8,128)S(1)}, u32[]{:S(2)}, u32[]{:S(2)}) collective-permute-start(f32[40,1024]{1,0:T(8,128)S(1)} %collective-permute-done.9.near_ref), channel_id=1, source_target_pairs={{0,3},{3,0},{1,2},{2,1},{4,7},{7,4},{5,6},{6,5},{8,11},{11,8},{9,1... | collective-permute-start | bytes 491528 | tf_op jit(solution)/shard_map/ppermute | solution.py:560
  81.7 24.5 %copy-start = (f32[144,256]{1,0:T(8,128)}, f32[144,256]{1,0:T(8,128)S(1)}, u32[]{:S(2)}) copy-start(f32[144,256]{1,0:T(8,128)S(1)} %add.19.mine1) | copy-start | bytes 442372
  81.7 24.5 %collective-permute-start.2 = (f32[144,256]{1,0:T(8,128)S(1)}, f32[144,256]{1,0:T(8,128)S(1)}, u32[]{:S(2)}, u32[]{:S(2)}) collective-permute-start(f32[144,256]{1,0:T(8,128)S(1)} %add.19.mine1), channel_id=1, source_target_pairs={{0,1},{1,0},{2,3},{3,2},{4,5},{5,4},{6,7},{7,6},{8,9},{9,8},{10,11... | collective-permute-start | bytes 442376 | tf_op jit(solution)/shard_map/ppermute | solution.py:559
  81.8 24.4 %copy-start.1 = (f32[144,256]{1,0:T(8,128)}, f32[144,256]{1,0:T(8,128)S(1)}, u32[]{:S(2)}) copy-start(f32[144,256]{1,0:T(8,128)S(1)} %add.21.mine0) | copy-start | bytes 442372
  81.8 24.4 %collective-permute-start.5 = (f32[144,256]{1,0:T(8,128)S(1)}, f32[144,256]{1,0:T(8,128)S(1)}, u32[]{:S(2)}, u32[]{:S(2)}) collective-permute-start(f32[144,256]{1,0:T(8,128)S(1)} %add.21.mine0), channel_id=1, source_target_pairs={{0,1},{1,0},{2,3},{3,2},{4,5},{5,4},{6,7},{7,6},{8,9},{9,8},{10,11... | collective-permute-start | bytes 442376 | tf_op jit(solution)/shard_map/ppermute | solution.py:559
  83.9 14.2 %copy-start.2 = (f32[88,256]{1,0:T(8,128)}, f32[88,256]{1,0:T(8,128)S(1)}, u32[]{:S(2)}) copy-start(f32[88,256]{1,0:T(8,128)S(1)} %add.23.mine) | copy-start | bytes 270340
  83.9 14.1 %collective-permute-start.8 = (f32[88,256]{1,0:T(8,128)S(1)}, f32[88,256]{1,0:T(8,128)S(1)}, u32[]{:S(2)}, u32[]{:S(2)}) collective-permute-start(f32[88,256]{1,0:T(8,128)S(1)} %add.23.mine), channel_id=1, source_target_pairs={{0,1},{1,0},{2,3},{3,2},{4,5},{5,4},{6,7},{7,6},{8,9},{9,8},{10,11... | collective-permute-start | bytes 270344 | tf_op jit(solution)/shard_map/ppermute | solution.py:559
  100.3 0.7 copy-start.6
  101.0 0.7 copy-start.7
  106.2 0.7 copy-start.8
  106.9 0.7 copy-start.9
  (2 other events, 1.3 us)
where the time goes:
time: 110 us; the launch traced here: 109 us
  Pallas kernels  41.8 us (38%)
  starting transfers between devices  27 us (25%)
  waiting for transfers between devices  24.1 us (22%)
  blocking collectives  9.98 us (9%)
  local copies, waits for them, and re-layouts  3.87 us (4%)
  other arithmetic  1.94 us (2%)
    ppermute x7, waiting for transfers between devices, local(): swap = lambda x: lax.ppermute(x, 'rep', [(0, 1), (1, 0), (2, 3), (3, 2)])  21.3 us
    pallas_call x1, Pallas kernels, local(): pl.pallas_call(functools.partial(forward_kernel, group, codes), grid=(ste...  16 us
    ppermute x5, starting transfers between devices, local(): mirror = lambda x: lax.ppermute(x, 'rep', [(0, 3), (3, 0), (1, 2), (2, 1)])  11.3 us
    ppermute x7, starting transfers between devices, local(): swap = lambda x: lax.ppermute(x, 'rep', [(0, 1), (1, 0), (2, 3), (3, 2)])  10.5 us
    all_gather x1, blocking collectives, local(): parts = lax.all_gather(partial, 'blk', axis=0, tiled=False)  9.98 us
    pallas_call x1, Pallas kernels, local(): keep1, send1, keep0, send0 = trunk_call(low, d2, h1, h0, code, w1t, w0t)  7.37 us
    pallas_call x1, Pallas kernels, local(): pl.pallas_call(functools.partial(color_kernel, group, tiles), grid=(steps...  6.58 us
    all_to_all x1, starting transfers between devices, local(): rays = lax.all_to_all(send, 'blk', split_axis=0, concat_axis=0, tiled=True)  5.2 us
  transfers between devices with their start and end apart: 13, of which 4 were waited for; matrix products, arithmetic and copies ran while one was open for 2% of the time, Pallas kernels for 8%

commit v1 on v0

--- a/solution.py
+++ b/solution.py
@@ -18,6 +18,7 @@
 VCODE = 32
 EDGE = 144
 DENSE = 131
+GROUP = 8
 
 ray_span = 2.0
 loss_scale = 0.03125
@@ -102,10 +103,40 @@
             out_ref[ids_ref[t, k]] = tile_ref[t]
 
 
+def forward_views(pack, codes, highs):
+    top = highs * codes
+    side = top + 512 + EDGE
+    return (
+        pack.at[side : side + 256, 0:64],
+        pack.at[top : top + 512, :],
+        pack.at[top + 512 : side, :],
+        pack.at[side : side + 128, 128:192],
+        pack.at[side + 128 : side + 144, 128:256],
+        pack.at[0:top, :],
+    )
+
+
+def backward_views(pack, codes):
+    return (
+        pack.at[0:256, :],
+        pack.at[256:512, :],
+        pack.at[512:768, 0:EDGE],
+        pack.at[768 : 768 + codes, 128:256],
+        pack.at[768:896, 0:16],
+    )
+
+
 def weight_kernel(
-    pos_ref, tw_ref, density_ref, feature_ref, view_ref, cw_ref, rad_ref, table_ref,
-    wp, wfd, wvc, wr, stack, w0t, w1t, wfdt, wct, wrt, pad, narrow,
+    center_ref, pos_ref, tw_ref, density_ref, feature_ref, view_ref, cw_ref, rad_ref, table_ref,
+    fore_ref, back_ref, spot_ref, pad, narrow,
 ):
+    codes = table_ref.shape[0]
+    wp, tw, wfd, wvc, wr, stack = forward_views(fore_ref, codes, table_ref.shape[1] // LOW)
+    w0t, w1t, wfdt, wct, wrt = backward_views(back_ref, codes)
+    for c in range(3):
+        spot_ref[c : c + 1, :] = jnp.full((1, TILE), center_ref[0, c], F32)
+    tw[0:256, :] = tw_ref[0]
+    tw[256:512, :] = tw_ref[1]
     pad[...] = jnp.zeros_like(pad)
     pad[0 : pos_ref.shape[0], :] = pos_ref[...].astype(F32)
     wp[...] = pad[...].T.astype(BF16)
@@ -125,7 +156,6 @@
     wfdt[...] = wfd[...].T
     w0t[...] = tw_ref[0].T
     w1t[...] = tw_ref[1].T
-    codes = table_ref.shape[0]
     for hi in range(table_ref.shape[1] // LOW):
         stack[hi * codes : (hi + 1) * codes, :] = table_ref[:, hi * LOW : (hi + 1) * LOW]
 
@@ -144,57 +174,61 @@
 def distance(rays, centers):
     total = 1.0
     for c in range(3):
-        offset = rays[:, c, :] - centers[0, c]
+        offset = rays[:, c, :] - centers[c : c + 1, :]
         total = total + offset * offset
     return total
 
 
 def forward_kernel(
-    group, codes, rays_ref, center_ref, wp, tw, wfd, wvc, wr, stack,
+    group, codes, rays_ref, center_ref, pack_ref,
     partial_ref, code_ref, h0_ref, h1_ref, h2_ref, shade_ref, vc_ref, density_ref, radiance_ref,
     dl_scr, rl_scr,
 ):
     step = pl.program_id(0)
-    highs = stack.shape[0] // codes
-    for j in range(group):
-        tile = step * group + j
-        at = slice(j * COLS, (j + 1) * COLS)
-        rays = rays_ref[tile]
-        points = []
-        for c in range(3):
-            base = rays[c : c + 1, :]
-            move = rays[3 + c : 4 + c, :]
-            points.append(
-                jnp.concatenate(
-                    [base + ((s + 0.5) * spacing) * move - center_ref[0, c] for s in range(SAMPLES)], 1
-                )
-            )
-        code = encode(points, FREQ, wp.shape[1]).astype(BF16)
-        code_ref[:, at] = code
-        h0 = softplus(dot(wp[...], code)).astype(BF16)
-        h0_ref[:, at] = h0
-        h1 = softplus(dot(tw[0], h0)).astype(BF16)
-        h1_ref[:, at] = h1
-        h2 = softplus(dot(tw[1], h1)).astype(BF16)
-        h2_ref[:, at] = h2
-        feature = dot(wfd[...], h2)
-        dl_scr[pl.ds(tile, 1), :] = feature[DENSE : DENSE + 1, :]
-        view = encode([rays[3 + c : 4 + c, :] for c in range(3)], VFREQ, VCODE)
-        ids = rays[6:7, :].astype(jnp.int32)
+    highs = (pack_ref.shape[0] - 768 - EDGE) // codes
+    wp, tw, wfd, wvc, wr, stack = forward_views(pack_ref, codes, highs)
+    tiles = range(group)
+    at = [slice(j * COLS, (j + 1) * COLS) for j in tiles]
+    rays = [rays_ref[step * group + j] for j in tiles]
+    vcs = []
+    for j in tiles:
+        ids = rays[j][6:7, :].astype(jnp.int32)
         low, high = ids & (LOW - 1), ids // LOW
         hit = (lax.broadcasted_iota(jnp.int32, (LOW, TILE), 0) == low).astype(F32).astype(BF16)
         picked = dot(stack[...], hit)
         app = jnp.zeros((codes, TILE), F32)
         for hi in range(highs):
             app = app + jnp.where(high == hi, picked[hi * codes : (hi + 1) * codes], 0.0)
-        vc = jnp.concatenate([app, view], 0).astype(BF16)
-        vc_ref[:, j * TILE : (j + 1) * TILE] = vc
-        per_ray = dot(wvc[...], vc)
+        view = encode([rays[j][3 + c : 4 + c, :] for c in range(3)], VFREQ, VCODE)
+        vcs.append(jnp.concatenate([app, view], 0).astype(BF16))
+        vc_ref[:, j * TILE : (j + 1) * TILE] = vcs[j]
+    for j in tiles:
+        points = []
+        for c in range(3):
+            base = rays[j][c : c + 1, :]
+            move = rays[j][3 + c : 4 + c, :]
+            points.append(
+                jnp.concatenate(
+                    [base + ((s + 0.5) * spacing) * move - center_ref[c : c + 1, :] for s in range(SAMPLES)], 1
+                )
+            )
+        code_ref[:, at[j]] = encode(points, FREQ, code_ref.shape[0]).astype(BF16)
+    for j in tiles:
+        h0_ref[:, at[j]] = softplus(dot(wp[...], code_ref[:, at[j]])).astype(BF16)
+    for j in tiles:
+        h1_ref[:, at[j]] = softplus(dot(tw[0:256, :], h0_ref[:, at[j]])).astype(BF16)
+    for j in tiles:
+        h2_ref[:, at[j]] = softplus(dot(tw[256:512, :], h1_ref[:, at[j]])).astype(BF16)
+    for j in tiles:
+        per_ray = dot(wvc[...], vcs[j])
+        feature = dot(wfd[...], h2_ref[:, at[j]])
+        dl_scr[pl.ds(step * group + j, 1), :] = feature[DENSE : DENSE + 1, :]
         shaded = softplus(feature[0:128] + jnp.concatenate([per_ray] * SAMPLES, 1)).astype(BF16)
-        shade_ref[:, at] = shaded
-        logits = dot(wr[...], shaded)
+        shade_ref[:, at[j]] = shaded
+    for j in tiles:
+        logits = dot(wr[...], shade_ref[:, at[j]])
         for c in range(3):
-            rl_scr[c, pl.ds(tile, 1), :] = logits[c : c + 1, :]
+            rl_scr[c, pl.ds(step * group + j, 1), :] = logits[c : c + 1, :]
 
     @pl.when(step == pl.num_programs(0) - 1)
     def _():
@@ -251,9 +285,9 @@
 
 def color_kernel(
     group, tiles, ids_ref, me_ref, rays_ref, center_ref, parts_ref, density_ref, radiance_ref,
-    h2_ref, shade_ref, vc_ref, wfdt, wct, wrt, low_ref,
+    h2_ref, shade_ref, vc_ref, pack_ref, low_ref,
     colors_ref, keep_ref, send_ref, column_ref, d2_ref,
-    cot_scr, head_ref, fd_scr, r_scr, vc_scr,
+    cot_scr, head_ref, fd_scr, r_scr, vc_scr, edge_scr,
 ):
     step = pl.program_id(0)
 
@@ -270,32 +304,37 @@
         for ref in (fd_scr, r_scr, vc_scr):
             ref[...] = jnp.zeros_like(ref)
 
-    for j in range(group):
-        tile = step * group + j
-        at = slice(j * COLS, (j + 1) * COLS)
-        cot = cot_scr[tile]
-        low = jnp.concatenate([cot, jnp.zeros_like(cot)], 0).astype(BF16)
-        shaded = shade_ref[:, at]
-        d_feature = dot(wrt[...], low) * slope(shaded)
-        r_scr[...] += dot_nt(low, shaded)
-        d_ray = (
-            d_feature[:, 0:TILE]
-            + d_feature[:, TILE : 2 * TILE]
-            + d_feature[:, 2 * TILE : 3 * TILE]
-            + d_feature[:, 3 * TILE :]
-        ).astype(BF16)
-        vc = vc_ref[:, j * TILE : (j + 1) * TILE]
-        vc_scr[...] += dot_nt(vc, d_ray)
+    codes = column_ref.shape[0] - 8
+    _, _, wfdt, wct, wrt = backward_views(pack_ref, codes)
+    each = range(group)
+    at = [slice(j * COLS, (j + 1) * COLS) for j in each]
+    lows, d_rays = [], []
+    for j in each:
+        cot = cot_scr[step * group + j]
+        lows.append(jnp.concatenate([cot, jnp.zeros_like(cot)], 0).astype(BF16))
+    for j in each:
+        d_feature = dot(wrt[...], lows[j]) * slope(shade_ref[:, at[j]])
+        d_rays.append(
+            (
+                d_feature[:, 0:TILE]
+                + d_feature[:, TILE : 2 * TILE]
+                + d_feature[:, 2 * TILE : 3 * TILE]
+                + d_feature[:, 3 * TILE :]
+            ).astype(BF16)
+        )
+        edge_scr[0:128, at[j]] = d_feature.astype(BF16)
+        edge_scr[128:EDGE, at[j]] = lows[j]
+    for j in each:
         lanes = slice(j * TILE, (j + 1) * TILE)
-        codes = wct.shape[0]
-        column_ref[0:codes, lanes] = dot(wct[...], d_ray).astype(BF16).astype(F32)
+        column_ref[0:codes, lanes] = dot(wct[...], d_rays[j]).astype(BF16).astype(F32)
         column_ref[codes:, lanes] = jnp.broadcast_to(
-            rays_ref[tile, 6:7, :], (column_ref.shape[0] - codes, TILE)
+            rays_ref[step * group + j, 6:7, :], (column_ref.shape[0] - codes, TILE)
         )
-        h2 = h2_ref[:, at]
-        edge = jnp.concatenate([d_feature.astype(BF16), low], 0)
-        fd_scr[...] += dot_nt(edge, h2)
-        d2_ref[:, at] = (dot(wfdt[...], edge) * slope(h2)).astype(BF16)
+    for j in each:
+        d2_ref[:, at[j]] = (dot(wfdt[...], edge_scr[:, at[j]]) * slope(h2_ref[:, at[j]])).astype(BF16)
+    r_scr[...] += dot_nt(edge_scr[128:EDGE, :], shade_ref[...])
+    vc_scr[...] += dot_nt(vc_ref[...], jnp.concatenate(d_rays, 1))
+    fd_scr[...] += dot_nt(edge_scr[...], h2_ref[...])
 
     @pl.when(step == pl.num_programs(0) - 1)
     def _():
@@ -315,25 +354,25 @@
 
 
 def trunk_kernel(
-    group, low_ref, d2_ref, h1_ref, h0_ref, code_ref, w1t, w0t,
-    keep1, send1, keep0, send0, grad,
+    group, low_ref, d2_ref, h1_ref, h0_ref, code_ref, pack_ref,
+    keep1, send1, keep0, send0, grad, d1_scr, d0_scr,
 ):
     step = pl.program_id(0)
-    hid = w1t.shape[0]
+    w0t, w1t = backward_views(pack_ref, 32)[0:2]
+    hid = d2_ref.shape[0]
 
     @pl.when(step == 0)
     def _():
         grad[...] = jnp.zeros_like(grad)
 
-    for j in range(group):
-        at = slice(j * COLS, (j + 1) * COLS)
-        d2, h1 = d2_ref[:, at], h1_ref[:, at]
-        grad[0:hid, :] += dot_nt(d2, h1)
-        d1 = (dot(w1t[...], d2) * slope(h1)).astype(BF16)
-        h0 = h0_ref[:, at]
-        grad[hid : 2 * hid, :] += dot_nt(d1, h0)
-        d0 = (dot(w0t[...], d1) * slope(h0)).astype(BF16)
-        grad[2 * hid :, :] += dot_nt(code_ref[:, at], d0)
+    at = [slice(j * COLS, (j + 1) * COLS) for j in range(group)]
+    for cols in at:
+        d1_scr[:, cols] = (dot(w1t[...], d2_ref[:, cols]) * slope(h1_ref[:, cols])).astype(BF16)
+    for cols in at:
+        d0_scr[:, cols] = (dot(w0t[...], d1_scr[:, cols]) * slope(h0_ref[:, cols])).astype(BF16)
+    grad[0:hid, :] += dot_nt(d2_ref[...], h1_ref[...])
+    grad[hid : 2 * hid, :] += dot_nt(d1_scr[...], h0_ref[...])
+    grad[2 * hid :, :] += dot_nt(code_ref[...], d0_scr[...])
 
     @pl.when(step == pl.num_programs(0) - 1)
     def _():
@@ -419,10 +458,12 @@
     blocks = lax.axis_size("blk")
     reps = lax.axis_size("rep")
     assert reps == 4
-    group = 2 if blocks % 2 == 0 else 1
+    group = next(g for g in (GROUP, 4, 2, 1) if blocks % g == 0)
     hid = pos_weight.shape[1]
     codes, entries = code_table.shape[1:]
-    params = pltpu.CompilerParams(vmem_limit_bytes=58 * 1024 * 1024)
+    params = pltpu.CompilerParams(vmem_limit_bytes=30000 * 1024)
+    alone = pltpu.CompilerParams(vmem_limit_bytes=60 * 1024 * 1024)
+    light = pltpu.CompilerParams(vmem_limit_bytes=8000 * 1024)
 
     send = pl.pallas_call(
         functools.partial(send_kernel, tiles),
@@ -430,31 +471,29 @@
         in_specs=[smem()] + [vmem()] * 4,
         out_specs=vmem(),
         scratch_shapes=[pltpu.VMEM((tiles, ROWS, TILE), F32)],
+        compiler_params=alone,
         name="send",
     )(block_ids, anchors, directions, app_ids.reshape(tiles, TILE), color_grad)
     rays = lax.all_to_all(send, "blk", split_axis=0, concat_axis=0, tiled=True)
 
-    trunk = trunk_weight[0]
     positions, views = pos_weight.shape[2], view_weight.shape[2]
-    wp, wfd, wvc, wr, stack, w0t, w1t, wfdt, wct, wrt = pl.pallas_call(
+    fore, back, centers = pl.pallas_call(
         weight_kernel,
-        out_shape=tuple(
-            shape_of(*dims, dtype=BF16)
-            for dims in (
-                (hid, 64), (EDGE, hid), (128, 64), (16, 128), (entries // LOW * codes, LOW),
-                (hid, hid), (hid, hid), (hid, EDGE), (codes, 128), (128, 16),
-            )
+        out_shape=(
+            shape_of(entries // LOW * codes + 768 + EDGE, hid, dtype=BF16),
+            shape_of(896, hid, dtype=BF16),
+            shape_of(8, TILE),
         ),
-        in_specs=[vmem()] * 8,
-        out_specs=(vmem(),) * 10,
+        in_specs=[smem()] + [vmem()] * 8,
+        out_specs=(vmem(),) * 3,
         scratch_shapes=[pltpu.VMEM((64, hid), F32), pltpu.VMEM((64, 128), F32)],
+        compiler_params=alone,
         name="weights",
     )(
-        pos_weight[0].T, trunk, density_weight, feature_weight[0], view_weight[0].T,
-        code_weight[0].T, radiance_weight[0], code_table[0],
-    )
-
-    centers = block_centers.T
+        block_centers.T, pos_weight[0].T, trunk_weight[0], density_weight, feature_weight[0],
+        view_weight[0].T, code_weight[0].T, radiance_weight[0], code_table[0],
+    )
+
     n = blocks * COLS
     steps = blocks // group
     wide = lambda rows, cols: pl.BlockSpec((rows, group * cols), lambda i: (0, i))
@@ -484,19 +523,14 @@
         out_shape=(shape_of(4, blocks, TILE),) + saved_shapes,
         in_specs=[
             whole(rays.shape),
-            smem(),
-            whole(wp.shape),
-            whole(trunk.shape),
-            whole(wfd.shape),
-            whole(wvc.shape),
-            whole(wr.shape),
-            whole(stack.shape),
+            whole(centers.shape),
+            whole(fore.shape),
         ],
         out_specs=(whole((4, blocks, TILE)),) + saved_specs,
         scratch_shapes=[pltpu.VMEM((blocks, COLS), F32), pltpu.VMEM((3, blocks, COLS), F32)],
         compiler_params=params,
         name="forward",
-    )(rays, centers, wp, trunk, wfd, wvc, wr, stack)
+    )(rays, centers, fore)
     partial, saved = outs[0], outs[1:]
     code, h0, h1, h2, shaded, vc, density, radiance = saved
     parts = lax.all_gather(partial, "blk", axis=0, tiled=False)
@@ -518,11 +552,10 @@
             shape_of(code_rows, blocks * TILE),
             shape_of(hid, n, dtype=BF16),
         ),
-        in_specs=[smem(), smem(), whole(rays.shape), smem(), whole(parts.shape)]
+        in_specs=[smem(), smem(), whole(rays.shape), whole(centers.shape), whole(parts.shape)]
         + [saved_specs[6], saved_specs[7]]
         + list(saved_specs[3:6])
-        + [whole(w.shape) for w in (wfdt, wct, wrt)]
-        + [smem()],
+        + [whole(back.shape), smem()],
         out_specs=(
             whole((3, tiles * TILE)),
             whole((head_rows // 2, hid)),
@@ -536,25 +569,27 @@
             pltpu.VMEM((EDGE, hid), F32),
             pltpu.VMEM((16, 128), F32),
             pltpu.VMEM((64, 128), F32),
+            pltpu.VMEM((EDGE, group * COLS), BF16),
         ],
         compiler_params=params,
         cost_estimate=square(hid, 4 * EDGE),
         name="color",
-    )(block_ids, me, rays, centers, parts, density, radiance, h2, shaded, vc, wfdt, wct, wrt, low)
+    )(block_ids, me, rays, centers, parts, density, radiance, h2, shaded, vc, back, low)
 
     part = half(trunk_rows, 2)
     trunk_call = pl.pallas_call(
         functools.partial(trunk_kernel, group),
         grid=(steps,),
         out_shape=(part,) * 4,
-        in_specs=[smem()] + [wide(x, COLS) for x in (hid, hid, hid, 64)] + [whole((hid, hid))] * 2,
+        in_specs=[smem()] + [wide(x, COLS) for x in (hid, hid, hid, 64)] + [whole(back.shape)],
         out_specs=(whole(part.shape),) * 4,
-        scratch_shapes=[pltpu.VMEM((trunk_rows, hid), F32)],
+        scratch_shapes=[pltpu.VMEM((trunk_rows, hid), F32)]
+        + [pltpu.VMEM((hid, group * COLS), BF16)] * 2,
         compiler_params=params,
         cost_estimate=square(hid, 8 * hid),
         name="trunk",
     )
-    keep1, send1, keep0, send0 = trunk_call(low, d2, h1, h0, code, w1t, w0t)
+    keep1, send1, keep0, send0 = trunk_call(low, d2, h1, h0, code, back)
 
     swap = lambda x: lax.ppermute(x, "rep", [(0, 1), (1, 0), (2, 3), (3, 2)])
     mirror = lambda x: lax.ppermute(x, "rep", [(0, 3), (3, 0), (1, 2), (2, 1)])
@@ -600,6 +635,7 @@
         in_specs=[smem()] + [vmem()] * 2,
         out_specs=(vmem(),) * 5,
         scratch_shapes=[pltpu.VMEM((head_rows, hid), F32)],
+        compiler_params=light,
         name="heads",
     )
     grad_density, grad_feature, grad_view, grad_code, grad_rad = heads_call(low, *head_sum)
@@ -609,6 +645,7 @@
         in_specs=[smem()] + [vmem()] * 4,
         out_specs=(vmem(),) * 2,
         scratch_shapes=[pltpu.VMEM((trunk_rows, hid), F32)],
+        compiler_params=light,
         name="sides",
     )(low, *sums)
     return (

time: 110 us -> 89.2 us (0.81)
  Pallas kernels: 41.8 us -> 23.9 us
  starting transfers between devices: 27 us -> 29.6 us
  other arithmetic: 1.94 us -> 0.11 us
  waiting for transfers between devices: 24.1 us -> 22.4 us
  blocking collectives: 9.98 us -> 8.44 us
    pallas_call x1, Pallas kernels: 16 us -> 7.95 us  [local(): pl.pallas_call(functools.partial(forward_kernel, group, codes), grid=(ste...]
    pallas_call x2, Pallas kernels: 9.7 us -> 6.14 us  [the longest x1 3.61 us: local(): keep1, send1, keep0, send0 = trunk_call(low, d2, h1, h0, code, back)]
    pallas_call x1, Pallas kernels: 6.58 us -> 3.45 us  [local(): pl.pallas_call(functools.partial(color_kernel, group, tiles), grid=(steps...]
    add x3, other arithmetic: 1.88 us -> 0.05 us  [rep_sum(): pair = keep + got]
    all_gather x1, blocking collectives: 9.98 us -> 8.44 us  [local(): parts = lax.all_gather(partial, 'blk', axis=0, tiled=False)]
    ppermute x7, waiting for transfers between devices: 21.3 us -> 19.9 us  [local(): swap = lambda x: lax.ppermute(x, 'rep', [(0, 1), (1, 0), (2, 3), (3, 2)])]
    ppermute x5, starting transfers between devices: 11.3 us -> 12.6 us  [local(): mirror = lambda x: lax.ppermute(x, 'rep', [(0, 3), (3, 0), (1, 2), (2, 1)])]
    ppermute x7, starting transfers between devices: 10.5 us -> 11.8 us  [local(): swap = lambda x: lax.ppermute(x, 'rep', [(0, 1), (1, 0), (2, 3), (3, 2)])]
  transfers between devices with their start and end apart: 13 -> 13, of which waited for: 4 -> 4; matrix products, arithmetic and copies ran while one was open for 2% -> 0% of each run, Pallas kernels for 8% -> 7%
where the time goes in v1:
time: 89.2 us; the launch traced here: 88.8 us
  starting transfers between devices  29.6 us (33%)
  Pallas kernels  23.9 us (27%)
  waiting for transfers between devices  22.4 us (25%)
  blocking collectives  8.44 us (9%)
  local copies, waits for them, and re-layouts  3.6 us (4%)
    ppermute x7, waiting for transfers between devices, local(): swap = lambda x: lax.ppermute(x, 'rep', [(0, 1), (1, 0), (2, 3), (3, 2)])  19.9 us
    ppermute x5, starting transfers between devices, local(): mirror = lambda x: lax.ppermute(x, 'rep', [(0, 3), (3, 0), (1, 2), (2, 1)])  12.6 us
    ppermute x7, starting transfers between devices, local(): swap = lambda x: lax.ppermute(x, 'rep', [(0, 1), (1, 0), (2, 3), (3, 2)])  11.8 us
    all_gather x1, blocking collectives, local(): parts = lax.all_gather(partial, 'blk', axis=0, tiled=False)  8.44 us
    pallas_call x1, Pallas kernels, local(): pl.pallas_call(functools.partial(forward_kernel, group, codes), grid=(ste...  7.95 us
    all_to_all x1, starting transfers between devices, local(): rays = lax.all_to_all(send, 'blk', split_axis=0, concat_axis=0, tiled=True)  5.2 us
    pallas_call x1, Pallas kernels, local(): keep1, send1, keep0, send0 = trunk_call(low, d2, h1, h0, code, back)  3.61 us
    unnamed x10, local copies, waits for them, and re-layouts  3.6 us
  transfers between devices with their start and end apart: 13, of which 4 were waited for; matrix products, arithmetic and copies ran while one was open for 0% of the time, Pallas kernels for 7%

profile of v1, /device:TPU:0, one launch (start us, length us, event | category | flops | bytes accessed | tf_op | source)
XLA Modules:
  0.0 88.8 jit_solution(9600882988194922009)
XLA Ops:
  0.7 1.5 %send.1 = f32[8,16,128]{2,1,0:T(8,128)} custom-call(s32[2,3]{1,0:T(2,128)} %ids_ref.3, f32[3,256]{1,0:T(4,128)} %anchor_ref.1, f32[3,256]{1,0:T(4,128)} %dir_ref.1, s32[2,128]{1,0:T(2,128)} %bitcast.35, f32[3,256]{1,0:T(4,128)} %grad_ref.1), custom_call_target="tpu_custom_call" | custom-call | tf_op jit(solution)/shard_map/send/pallas_call | solution.py:468
  2.1 5.2 %all-to-all-start = ((f32[8,16,128]{2,1,0:T(8,128)}), f32[8,16,128]{2,1,0:T(8,128)S(1)}, u32[]{:S(2)}, u32[]{:S(2)}) async-start(f32[8,16,128]{2,1,0:T(8,128)} %send.1), calls=%async_computation | async-start | bytes 131072 | tf_op jit(solution)/shard_map/all_to_all | solution.py:477
  7.3 2.5 %weights.1 = (bf16[1936,256]{1,0:T(8,128)(2,1)}, bf16[896,256]{1,0:T(8,128)(2,1)}, f32[8,128]{1,0:T(8,128)}) custom-call(f32[1,3]{1,0:T(1,128)} %bitcast.37, bf16[63,256]{1,0:T(8,128)(2,1)} %bitcast.32, bf16[2,256,256]{2,1,0:T(8,128)(2,1)} %bitcast.30, bf16[1,256]{1,0:T(2,128)(2,1)} %density_ref.1, bf16[128,256]{1,0:T(8,128)(2,1)} %bitcast.31, ...), custom_call_target="tpu_custom_call" | custom-call | tf_op jit(solution)/shard_map/weights/pallas_call | solution.py:480
  9.9 2.5 %all-to-all-done.rays_ref = f32[8,16,128]{2,1,0:T(8,128)S(1)} async-done(((f32[8,16,128]{2,1,0:T(8,128)}), f32[8,16,128]{2,1,0:T(8,128)S(1)}, u32[]{:S(2)}, u32[]{:S(2)}) %all-to-all-start) | async-done | bytes 65568 | tf_op jit(solution)/shard_map/all_to_all | solution.py:477
  12.3 1.2 %copy-done = bf16[1936,256]{1,0:T(8,128)(2,1)S(1)} copy-done((bf16[1936,256]{1,0:T(8,128)(2,1)S(1)}, bf16[1936,256]{1,0:T(8,128)(2,1)}, u32[]{:S(2)}) %copy-start) | copy-done | bytes 991256
  14.2 8.0 %forward.1 = (f32[4,8,128]{2,1,0:T(8,128)S(1)}, bf16[64,4096]{1,0:T(8,128)(2,1)S(1)}, bf16[256,4096]{1,0:T(8,128)(2,1)S(1)}, bf16[256,4096]{1,0:T(8,128)(2,1)S(1...) custom-call(f32[8,16,128]{2,1,0:T(8,128)S(1)} %all-to-all-done.rays_, ...), custom_call_target="tpu_custom_call" | custom-call | tf_op jit(solution)/shard_map/forward/pallas_call | solution.py:520
  22.2 8.4 %all-gather = f32[32,8,128]{2,1,0:T(8,128)S(1)} all-gather(f32[4,8,128]{2,1,0:T(8,128)S(1)} %get-tuple-element.39), channel_id=2, replica_groups=mesh['blk'=8,'rep'=4] {'blk'}, dimensions={0}, use_global_device_ids=true | all-gather | bytes 147456 | tf_op jit(solution)/shard_map/all_gather | solution.py:536
  31.3 1.0 %copy-done.4 = bf16[896,256]{1,0:T(8,128)(2,1)S(1)} copy-done((bf16[896,256]{1,0:T(8,128)(2,1)S(1)}, bf16[896,256]{1,0:T(8,128)(2,1)}, u32[]{:S(2)}) %copy-start.4) | copy-done | bytes 458776
  32.3 3.4 %color.1 = (f32[3,256]{1,0:T(4,128)}, f32[88,256]{1,0:T(8,128)S(1)}, f32[88,256]{1,0:T(8,128)S(1)}, f32[40,1024]{1,0:T(8,128)S(1)}, bf16[256,4096]{1,0:T(8,128)(2,1)S(1)}) custom-call(s32[2,3]{1,0:T(2,128)S(1)} %copy-done.3, s32[1]{0:T(128)} %bitcast.me_ref, f32[8,16,128]{2,1,0:T(8,128)S(1)} %all-to-all-done.rays_ref, f32[8,128]{1,0:T(8,128)S(1)} %copy-done.2, ...), custom_call_target="tpu_custom_call" | custom-call | flops 1207959552 | bytes 2097152 | tf_op jit(solution)/shard_map/color/pallas_call | solution.py:545
  35.8 3.6 %trunk.1 = (f32[144,256]{1,0:T(8,128)S(1)}, f32[144,256]{1,0:T(8,128)S(1)}, f32[144,256]{1,0:T(8,128)S(1)}, f32[144,256]{1,0:T(8,128)S(1)}) custom-call(s32[1]{0:T(128)S(6)} %convert_element_type.3.low_ref, bf16[256,4096]{1,0:T(8,128)(2,1)S(1)} %get-tuple-element.47.d2_ref, bf16[256,4096]{1,0:T(8,128)(2,1)S(1)} %get-tuple-element.48.h1_ref, ...), custom_call_target="tpu_custom_call" | custom-call | flops 4294967296 | bytes 2097152 | tf_op jit(solution)/shard_map/trunk/pallas_call | solution.py:592
  39.4 1.6 %collective-permute-start = (f32[144,256]{1,0:T(8,128)S(1)}, f32[144,256]{1,0:T(8,128)S(1)}, u32[]{:S(2)}, u32[]{:S(2)}) collective-permute-start(f32[144,256]{1,0:T(8,128)S(1)} %get-tuple-element.52), channel_id=1, source_target_pairs={{0,1},{1,0},{2,3},{3,2},{4,5},{5,4},{6,7},{7,6},{8,9},{9,8},{10,11... | collective-permute-start | bytes 442376 | tf_op jit(solution)/shard_map/ppermute | solution.py:594
  41.5 1.6 %collective-permute-start.9 = (f32[40,1024]{1,0:T(8,128)S(1)}, f32[40,1024]{1,0:T(8,128)S(1)}, u32[]{:S(2)}, u32[]{:S(2)}) collective-permute-start(f32[40,1024]{1,0:T(8,128)S(1)} %get-tuple-element.64.own_ref), channel_id=1, source_target_pairs={{0,1},{1,0},{2,3},{3,2},{4,5},{5,4},{6,7},{7,6},{8,9},{9,8},{10,11... | collective-permute-start | bytes 491528 | tf_op jit(solution)/shard_map/ppermute | solution.py:594
  43.1 3.1 %collective-permute-done = f32[144,256]{1,0:T(8,128)S(1)} collective-permute-done((f32[144,256]{1,0:T(8,128)S(1)}, f32[144,256]{1,0:T(8,128)S(1)}, u32[]{:S(2)}, u32[]{:S(2)}) %collective-permute-start) | collective-permute-done | bytes 147488 | tf_op jit(solution)/shard_map/ppermute | solution.py:594
  46.2 3.7 %collective-permute-start.1 = (f32[144,256]{1,0:T(8,128)S(1)}, f32[144,256]{1,0:T(8,128)S(1)}, u32[]{:S(2)}, u32[]{:S(2)}) collective-permute-start(f32[144,256]{1,0:T(8,128)S(1)} %add.18), channel_id=1, source_target_pairs={{0,3},{3,0},{1,2},{2,1},{4,7},{7,4},{5,6},{6,5},{8,11},{11,8},{9,1... | collective-permute-start | bytes 442376 | tf_op jit(solution)/shard_map/ppermute | solution.py:595
  49.9 3.1 %collective-permute-start.4 = (f32[144,256]{1,0:T(8,128)S(1)}, f32[144,256]{1,0:T(8,128)S(1)}, u32[]{:S(2)}, u32[]{:S(2)}) collective-permute-start(f32[144,256]{1,0:T(8,128)S(1)} %add.20), channel_id=1, source_target_pairs={{0,3},{3,0},{1,2},{2,1},{4,7},{7,4},{5,6},{6,5},{8,11},{11,8},{9,1... | collective-permute-start | bytes 442376 | tf_op jit(solution)/shard_map/ppermute | solution.py:595
  53.1 9.1 %collective-permute-done.6 = f32[88,256]{1,0:T(8,128)S(1)} collective-permute-done((f32[88,256]{1,0:T(8,128)S(1)}, f32[88,256]{1,0:T(8,128)S(1)}, u32[]{:S(2)}, u32[]{:S(2)}) %collective-permute-start.6) | collective-permute-done | bytes 90144 | tf_op jit(solution)/shard_map/ppermute | solution.py:594
  62.2 2.0 %collective-permute-start.7 = (f32[88,256]{1,0:T(8,128)S(1)}, f32[88,256]{1,0:T(8,128)S(1)}, u32[]{:S(2)}, u32[]{:S(2)}) collective-permute-start(f32[88,256]{1,0:T(8,128)S(1)} %add.22), channel_id=1, source_target_pairs={{0,3},{3,0},{1,2},{2,1},{4,7},{7,4},{5,6},{6,5},{8,11},{11,8},{9,1... | collective-permute-start | bytes 270344 | tf_op jit(solution)/shard_map/ppermute | solution.py:595
  64.2 1.9 %collective-permute-start.10 = (f32[40,1024]{1,0:T(8,128)S(1)}, f32[40,1024]{1,0:T(8,128)S(1)}, u32[]{:S(2)}, u32[]{:S(2)}) collective-permute-start(f32[40,1024]{1,0:T(8,128)S(1)} %get-tuple-element.64.own_ref), channel_id=1, source_target_pairs={{0,3},{3,0},{1,2},{2,1},{4,7},{7,4},{5,6},{6,5},{8,11},{11,8},{9,1... | collective-permute-start | bytes 491528 | tf_op jit(solution)/shard_map/ppermute | solution.py:595
  66.1 1.9 %collective-permute-start.11 = (f32[40,1024]{1,0:T(8,128)S(1)}, f32[40,1024]{1,0:T(8,128)S(1)}, u32[]{:S(2)}, u32[]{:S(2)}) collective-permute-start(f32[40,1024]{1,0:T(8,128)S(1)} %collective-permute-done.9.near_ref), channel_id=1, source_target_pairs={{0,3},{3,0},{1,2},{2,1},{4,7},{7,4},{5,6},{6,5},{8,11},{11,8},{9,1... | collective-permute-start | bytes 491528 | tf_op jit(solution)/shard_map/ppermute | solution.py:595
  68.2 2.1 %collective-permute-start.5 = (f32[144,256]{1,0:T(8,128)S(1)}, f32[144,256]{1,0:T(8,128)S(1)}, u32[]{:S(2)}, u32[]{:S(2)}) collective-permute-start(f32[144,256]{1,0:T(8,128)S(1)} %add.21.mine0), channel_id=1, source_target_pairs={{0,1},{1,0},{2,3},{3,2},{4,5},{5,4},{6,7},{7,6},{8,9},{9,8},{10,11... | collective-permute-start | bytes 442376 | tf_op jit(solution)/shard_map/ppermute | solution.py:594
  70.2 6.0 %collective-permute-start.8 = (f32[88,256]{1,0:T(8,128)S(1)}, f32[88,256]{1,0:T(8,128)S(1)}, u32[]{:S(2)}, u32[]{:S(2)}) collective-permute-start(f32[88,256]{1,0:T(8,128)S(1)} %add.23.mine), channel_id=1, source_target_pairs={{0,1},{1,0},{2,3},{3,2},{4,5},{5,4},{6,7},{7,6},{8,9},{9,8},{10,11... | collective-permute-start | bytes 270344 | tf_op jit(solution)/shard_map/ppermute | solution.py:594
  76.2 7.6 %collective-permute-done.8.other = f32[88,256]{1,0:T(8,128)S(1)} collective-permute-done((f32[88,256]{1,0:T(8,128)S(1)}, f32[88,256]{1,0:T(8,128)S(1)}, u32[]{:S(2)}, u32[]{:S(2)}) %collective-permute-start.8) | collective-permute-done | bytes 90144 | tf_op jit(solution)/shard_map/ppermute | solution.py:594
  84.6 3.4 %table.1 = f32[32,8192]{1,0:T(8,128)} custom-call(s32[1]{0:T(128)} %bitcast.14.side_ref, f32[40,1024]{1,0:T(8,128)S(1)} %get-tuple-element.64.own_ref, f32[40,1024]{1,0:T(8,128)S(1)} %collective-permute-done.9.near_ref, f32[40,1024]{1,0:T(8,128)S(1)} %collective-permute-done.10.far0_ref, f32[40,1024]{1,0:T(8,128)S(1)} %collective-permute-done.11.far1_ref), custom_call_target="tpu_custom_call" | custom-call | tf_op jit(solution)/shard_map/table/pallas_call | solution.py:624
  88.0 0.8 sides.1
  (27 shorter events, 2.7 us)
Async XLA Ops:
  0.6 30.0 %copy-start.3 = (s32[2,3]{1,0:T(2,128)S(1)}, s32[2,3]{1,0:T(2,128)}, u32[]{:S(2)}) copy-start(s32[2,3]{1,0:T(2,128)} %ids_ref.3) | copy-start | bytes 76
  2.1 10.2 %all-to-all-start = ((f32[8,16,128]{2,1,0:T(8,128)}), f32[8,16,128]{2,1,0:T(8,128)S(1)}, u32[]{:S(2)}, u32[]{:S(2)}) async-start(f32[8,16,128]{2,1,0:T(8,128)} %send.1), calls=%async_computation | async-start | bytes 131072 | tf_op jit(solution)/shard_map/all_to_all | solution.py:477
  12.3 1.2 %copy-start = (bf16[1936,256]{1,0:T(8,128)(2,1)S(1)}, bf16[1936,256]{1,0:T(8,128)(2,1)}, u32[]{:S(2)}) copy-start(bf16[1936,256]{1,0:T(8,128)(2,1)} %get-tuple-element.38.pack_ref) | copy-start | bytes 2973700
  13.6 0.7 copy-start.1
  30.6 0.7 copy-start.2
  31.3 1.0 %copy-start.4 = (bf16[896,256]{1,0:T(8,128)(2,1)S(1)}, bf16[896,256]{1,0:T(8,128)(2,1)}, u32[]{:S(2)}) copy-start(bf16[896,256]{1,0:T(8,128)(2,1)} %get-tuple-element.45.pack_ref) | copy-start | bytes 1376260
  39.4 6.8 %collective-permute-start = (f32[144,256]{1,0:T(8,128)S(1)}, f32[144,256]{1,0:T(8,128)S(1)}, u32[]{:S(2)}, u32[]{:S(2)}) collective-permute-start(f32[144,256]{1,0:T(8,128)S(1)} %get-tuple-element.52), channel_id=1, source_target_pairs={{0,1},{1,0},{2,3},{3,2},{4,5},{5,4},{6,7},{7,6},{8,9},{9,8},{10,11... | collective-permute-start | bytes 442376 | tf_op jit(solution)/shard_map/ppermute | solution.py:594
  41.1 8.8 %collective-permute-start.3 = (f32[144,256]{1,0:T(8,128)S(1)}, f32[144,256]{1,0:T(8,128)S(1)}, u32[]{:S(2)}, u32[]{:S(2)}) collective-permute-start(f32[144,256]{1,0:T(8,128)S(1)} %get-tuple-element.54), channel_id=1, source_target_pairs={{0,1},{1,0},{2,3},{3,2},{4,5},{5,4},{6,7},{7,6},{8,9},{9,8},{10,11... | collective-permute-start | bytes 442376 | tf_op jit(solution)/shard_map/ppermute | solution.py:594
  41.5 24.6 %collective-permute-start.9 = (f32[40,1024]{1,0:T(8,128)S(1)}, f32[40,1024]{1,0:T(8,128)S(1)}, u32[]{:S(2)}, u32[]{:S(2)}) collective-permute-start(f32[40,1024]{1,0:T(8,128)S(1)} %get-tuple-element.64.own_ref), channel_id=1, source_target_pairs={{0,1},{1,0},{2,3},{3,2},{4,5},{5,4},{6,7},{7,6},{8,9},{9,8},{10,11... | collective-permute-start | bytes 491528 | tf_op jit(solution)/shard_map/ppermute | solution.py:594
  46.2 21.8 %collective-permute-start.1 = (f32[144,256]{1,0:T(8,128)S(1)}, f32[144,256]{1,0:T(8,128)S(1)}, u32[]{:S(2)}, u32[]{:S(2)}) collective-permute-start(f32[144,256]{1,0:T(8,128)S(1)} %add.18), channel_id=1, source_target_pairs={{0,3},{3,0},{1,2},{2,1},{4,7},{7,4},{5,6},{6,5},{8,11},{11,8},{9,1... | collective-permute-start | bytes 442376 | tf_op jit(solution)/shard_map/ppermute | solution.py:595
  49.9 18.2 %collective-permute-start.4 = (f32[144,256]{1,0:T(8,128)S(1)}, f32[144,256]{1,0:T(8,128)S(1)}, u32[]{:S(2)}, u32[]{:S(2)}) collective-permute-start(f32[144,256]{1,0:T(8,128)S(1)} %add.20), channel_id=1, source_target_pairs={{0,3},{3,0},{1,2},{2,1},{4,7},{7,4},{5,6},{6,5},{8,11},{11,8},{9,1... | collective-permute-start | bytes 442376 | tf_op jit(solution)/shard_map/ppermute | solution.py:595
  53.1 9.1 %collective-permute-start.6 = (f32[88,256]{1,0:T(8,128)S(1)}, f32[88,256]{1,0:T(8,128)S(1)}, u32[]{:S(2)}, u32[]{:S(2)}) collective-permute-start(f32[88,256]{1,0:T(8,128)S(1)} %get-tuple-element.58), channel_id=1, source_target_pairs={{0,1},{1,0},{2,3},{3,2},{4,5},{5,4},{6,7},{7,6},{8,9},{9,8},{10,11... | collective-permute-start | bytes 270344 | tf_op jit(solution)/shard_map/ppermute | solution.py:594
  62.2 8.0 %collective-permute-start.7 = (f32[88,256]{1,0:T(8,128)S(1)}, f32[88,256]{1,0:T(8,128)S(1)}, u32[]{:S(2)}, u32[]{:S(2)}) collective-permute-start(f32[88,256]{1,0:T(8,128)S(1)} %add.22), channel_id=1, source_target_pairs={{0,3},{3,0},{1,2},{2,1},{4,7},{7,4},{5,6},{6,5},{8,11},{11,8},{9,1... | collective-permute-start | bytes 270344 | tf_op jit(solution)/shard_map/ppermute | solution.py:595
  64.2 20.4 %collective-permute-start.10 = (f32[40,1024]{1,0:T(8,128)S(1)}, f32[40,1024]{1,0:T(8,128)S(1)}, u32[]{:S(2)}, u32[]{:S(2)}) collective-permute-start(f32[40,1024]{1,0:T(8,128)S(1)} %get-tuple-element.64.own_ref), channel_id=1, source_target_pairs={{0,3},{3,0},{1,2},{2,1},{4,7},{7,4},{5,6},{6,5},{8,11},{11,8},{9,1... | collective-permute-start | bytes 491528 | tf_op jit(solution)/shard_map/ppermute | solution.py:595
  66.1 18.5 %collective-permute-start.11 = (f32[40,1024]{1,0:T(8,128)S(1)}, f32[40,1024]{1,0:T(8,128)S(1)}, u32[]{:S(2)}, u32[]{:S(2)}) collective-permute-start(f32[40,1024]{1,0:T(8,128)S(1)} %collective-permute-done.9.near_ref), channel_id=1, source_target_pairs={{0,3},{3,0},{1,2},{2,1},{4,7},{7,4},{5,6},{6,5},{8,11},{11,8},{9,1... | collective-permute-start | bytes 491528 | tf_op jit(solution)/shard_map/ppermute | solution.py:595
  68.0 19.9 %collective-permute-start.2 = (f32[144,256]{1,0:T(8,128)S(1)}, f32[144,256]{1,0:T(8,128)S(1)}, u32[]{:S(2)}, u32[]{:S(2)}) collective-permute-start(f32[144,256]{1,0:T(8,128)S(1)} %add.19.mine1), channel_id=1, source_target_pairs={{0,1},{1,0},{2,3},{3,2},{4,5},{5,4},{6,7},{7,6},{8,9},{9,8},{10,11... | collective-permute-start | bytes 442376 | tf_op jit(solution)/shard_map/ppermute | solution.py:594
  68.2 19.8 %collective-permute-start.5 = (f32[144,256]{1,0:T(8,128)S(1)}, f32[144,256]{1,0:T(8,128)S(1)}, u32[]{:S(2)}, u32[]{:S(2)}) collective-permute-start(f32[144,256]{1,0:T(8,128)S(1)} %add.21.mine0), channel_id=1, source_target_pairs={{0,1},{1,0},{2,3},{3,2},{4,5},{5,4},{6,7},{7,6},{8,9},{9,8},{10,11... | collective-permute-start | bytes 442376 | tf_op jit(solution)/shard_map/ppermute | solution.py:594
  70.2 13.6 %collective-permute-start.8 = (f32[88,256]{1,0:T(8,128)S(1)}, f32[88,256]{1,0:T(8,128)S(1)}, u32[]{:S(2)}, u32[]{:S(2)}) collective-permute-start(f32[88,256]{1,0:T(8,128)S(1)} %add.23.mine), channel_id=1, source_target_pairs={{0,1},{1,0},{2,3},{3,2},{4,5},{5,4},{6,7},{7,6},{8,9},{9,8},{10,11... | collective-permute-start | bytes 270344 | tf_op jit(solution)/shard_map/ppermute | solution.py:594

commit v2 on v1

--- a/solution.py
+++ b/solution.py
@@ -117,22 +117,23 @@
 
 
 def backward_views(pack, codes):
+    at = pack.shape[0] - 896
     return (
-        pack.at[0:256, :],
-        pack.at[256:512, :],
-        pack.at[512:768, 0:EDGE],
-        pack.at[768 : 768 + codes, 128:256],
-        pack.at[768:896, 0:16],
+        pack.at[at : at + 256, :],
+        pack.at[at + 256 : at + 512, :],
+        pack.at[at + 512 : at + 768, 0:EDGE],
+        pack.at[at + 768 : at + 768 + codes, 128:256],
+        pack.at[at + 768 : at + 896, 0:16],
     )
 
 
 def weight_kernel(
     center_ref, pos_ref, tw_ref, density_ref, feature_ref, view_ref, cw_ref, rad_ref, table_ref,
-    fore_ref, back_ref, spot_ref, pad, narrow,
+    pack_ref, spot_ref, pad, narrow,
 ):
     codes = table_ref.shape[0]
-    wp, tw, wfd, wvc, wr, stack = forward_views(fore_ref, codes, table_ref.shape[1] // LOW)
-    w0t, w1t, wfdt, wct, wrt = backward_views(back_ref, codes)
+    wp, tw, wfd, wvc, wr, stack = forward_views(pack_ref, codes, table_ref.shape[1] // LOW)
+    w0t, w1t, wfdt, wct, wrt = backward_views(pack_ref, codes)
     for c in range(3):
         spot_ref[c : c + 1, :] = jnp.full((1, TILE), center_ref[0, c], F32)
     tw[0:256, :] = tw_ref[0]
@@ -185,7 +186,7 @@
     dl_scr, rl_scr,
 ):
     step = pl.program_id(0)
-    highs = (pack_ref.shape[0] - 768 - EDGE) // codes
+    highs = (pack_ref.shape[0] - 896 - 768 - EDGE) // codes
     wp, tw, wfd, wvc, wr, stack = forward_views(pack_ref, codes, highs)
     tiles = range(group)
     at = [slice(j * COLS, (j + 1) * COLS) for j in tiles]
@@ -477,15 +478,14 @@
     rays = lax.all_to_all(send, "blk", split_axis=0, concat_axis=0, tiled=True)
 
     positions, views = pos_weight.shape[2], view_weight.shape[2]
-    fore, back, centers = pl.pallas_call(
+    pack, centers = pl.pallas_call(
         weight_kernel,
         out_shape=(
-            shape_of(entries // LOW * codes + 768 + EDGE, hid, dtype=BF16),
-            shape_of(896, hid, dtype=BF16),
+            shape_of(entries // LOW * codes + 768 + EDGE + 896, hid, dtype=BF16),
             shape_of(8, TILE),
         ),
         in_specs=[smem()] + [vmem()] * 8,
-        out_specs=(vmem(),) * 3,
+        out_specs=(vmem(),) * 2,
         scratch_shapes=[pltpu.VMEM((64, hid), F32), pltpu.VMEM((64, 128), F32)],
         compiler_params=alone,
         name="weights",
@@ -524,13 +524,13 @@
         in_specs=[
             whole(rays.shape),
             whole(centers.shape),
-            whole(fore.shape),
+            whole(pack.shape),
         ],
         out_specs=(whole((4, blocks, TILE)),) + saved_specs,
         scratch_shapes=[pltpu.VMEM((blocks, COLS), F32), pltpu.VMEM((3, blocks, COLS), F32)],
         compiler_params=params,
         name="forward",
-    )(rays, centers, fore)
+    )(rays, centers, pack)
     partial, saved = outs[0], outs[1:]
     code, h0, h1, h2, shaded, vc, density, radiance = saved
     parts = lax.all_gather(partial, "blk", axis=0, tiled=False)
@@ -555,7 +555,7 @@
         in_specs=[smem(), smem(), whole(rays.shape), whole(centers.shape), whole(parts.shape)]
         + [saved_specs[6], saved_specs[7]]
         + list(saved_specs[3:6])
-        + [whole(back.shape), smem()],
+        + [whole(pack.shape), smem()],
         out_specs=(
             whole((3, tiles * TILE)),
             whole((head_rows // 2, hid)),
@@ -574,14 +574,14 @@
         compiler_params=params,
         cost_estimate=square(hid, 4 * EDGE),
         name="color",
-    )(block_ids, me, rays, centers, parts, density, radiance, h2, shaded, vc, back, low)
+    )(block_ids, me, rays, centers, parts, density, radiance, h2, shaded, vc, pack, low)
 
     part = half(trunk_rows, 2)
     trunk_call = pl.pallas_call(
         functools.partial(trunk_kernel, group),
         grid=(steps,),
         out_shape=(part,) * 4,
-        in_specs=[smem()] + [wide(x, COLS) for x in (hid, hid, hid, 64)] + [whole(back.shape)],
+        in_specs=[smem()] + [wide(x, COLS) for x in (hid, hid, hid, 64)] + [whole(pack.shape)],
         out_specs=(whole(part.shape),) * 4,
         scratch_shapes=[pltpu.VMEM((trunk_rows, hid), F32)]
         + [pltpu.VMEM((hid, group * COLS), BF16)] * 2,
@@ -589,7 +589,7 @@
         cost_estimate=square(hid, 8 * hid),
         name="trunk",
     )
-    keep1, send1, keep0, send0 = trunk_call(low, d2, h1, h0, code, back)
+    keep1, send1, keep0, send0 = trunk_call(low, d2, h1, h0, code, pack)
 
     swap = lambda x: lax.ppermute(x, "rep", [(0, 1), (1, 0), (2, 3), (3, 2)])
     mirror = lambda x: lax.ppermute(x, "rep", [(0, 3), (3, 0), (1, 2), (2, 1)])

time: 89.2 us -> 87.9 us (0.985)
  local copies, waits for them, and re-layouts: 3.6 us -> 2.06 us
    unnamed x10 -> x8, local copies, waits for them, and re-layouts: 3.6 us -> 2.06 us
  transfers between devices with their start and end apart: 13 -> 13, of which waited for: 4 -> 4; matrix products, arithmetic and copies ran while one was open for 0% -> 0% of each run, Pallas kernels for 7% -> 8%
where the time goes in v2:
time: 87.9 us; the launch traced here: 87.5 us
  starting transfers between devices  29.6 us (34%)
  Pallas kernels  24.2 us (28%)
  waiting for transfers between devices  22.4 us (25%)
  blocking collectives  8.44 us (10%)
  local copies, waits for them, and re-layouts  2.06 us (2%)
    ppermute x7, waiting for transfers between devices, local(): swap = lambda x: lax.ppermute(x, 'rep', [(0, 1), (1, 0), (2, 3), (3, 2)])  20 us
    ppermute x5, starting transfers between devices, local(): mirror = lambda x: lax.ppermute(x, 'rep', [(0, 3), (3, 0), (1, 2), (2, 1)])  12.6 us
    ppermute x7, starting transfers between devices, local(): swap = lambda x: lax.ppermute(x, 'rep', [(0, 1), (1, 0), (2, 3), (3, 2)])  11.8 us
    all_gather x1, blocking collectives, local(): parts = lax.all_gather(partial, 'blk', axis=0, tiled=False)  8.44 us
    pallas_call x1, Pallas kernels, local(): pl.pallas_call(functools.partial(forward_kernel, group, codes), grid=(ste...  7.99 us
    all_to_all x1, starting transfers between devices, local(): rays = lax.all_to_all(send, 'blk', split_axis=0, concat_axis=0, tiled=True)  5.2 us
    pallas_call x1, Pallas kernels, local(): keep1, send1, keep0, send0 = trunk_call(low, d2, h1, h0, code, pack)  3.7 us
    pallas_call x1, Pallas kernels, local(): pl.pallas_call(functools.partial(color_kernel, group, tiles), grid=(steps...  3.54 us
  transfers between devices with their start and end apart: 13, of which 4 were waited for; matrix products, arithmetic and copies ran while one was open for 0% of the time, Pallas kernels for 8%

profile of v2, /device:TPU:0, one launch (start us, length us, event | category | flops | bytes accessed | tf_op | source)
XLA Modules:
  0.0 87.5 jit_solution(10369391722371385156)
XLA Ops:
  0.7 1.5 %send.1 = f32[8,16,128]{2,1,0:T(8,128)} custom-call(s32[2,3]{1,0:T(2,128)} %ids_ref.3, f32[3,256]{1,0:T(4,128)} %anchor_ref.1, f32[3,256]{1,0:T(4,128)} %dir_ref.1, s32[2,128]{1,0:T(2,128)} %bitcast.35, f32[3,256]{1,0:T(4,128)} %grad_ref.1), custom_call_target="tpu_custom_call" | custom-call | tf_op jit(solution)/shard_map/send/pallas_call | solution.py:469
  2.1 5.2 %all-to-all-start = ((f32[8,16,128]{2,1,0:T(8,128)}), f32[8,16,128]{2,1,0:T(8,128)S(1)}, u32[]{:S(2)}, u32[]{:S(2)}) async-start(f32[8,16,128]{2,1,0:T(8,128)} %send.1), calls=%async_computation | async-start | bytes 131072 | tf_op jit(solution)/shard_map/all_to_all | solution.py:478
  7.3 2.6 %weights.1 = (bf16[2832,256]{1,0:T(8,128)(2,1)}, f32[8,128]{1,0:T(8,128)}) custom-call(f32[1,3]{1,0:T(1,128)} %bitcast.37, bf16[63,256]{1,0:T(8,128)(2,1)} %bitcast.32, bf16[2,256,256]{2,1,0:T(8,128)(2,1)} %bitcast.30, bf16[1,256]{1,0:T(2,128)(2,1)} %density_ref.1, bf16[128,256]{1,0:T(8,128)(2,1)} %bitcast.31, bf16[27,128]{1,0:T(8,128)(2,1)} %bitcast.33, ...), custom_call_target="tpu_custom_call" | custom-call | tf_op jit(solution)/shard_map/weights/pallas_call | solution.py:481
  9.9 2.4 %all-to-all-done.rays_ref = f32[8,16,128]{2,1,0:T(8,128)S(1)} async-done(((f32[8,16,128]{2,1,0:T(8,128)}), f32[8,16,128]{2,1,0:T(8,128)S(1)}, u32[]{:S(2)}, u32[]{:S(2)}) %all-to-all-start) | async-done | bytes 65568 | tf_op jit(solution)/shard_map/all_to_all | solution.py:478
  12.3 1.4 %copy-done = bf16[2832,256]{1,0:T(8,128)(2,1)S(1)} copy-done((bf16[2832,256]{1,0:T(8,128)(2,1)S(1)}, bf16[2832,256]{1,0:T(8,128)(2,1)}, u32[]{:S(2)}) %copy-start) | copy-done | bytes 1450008
  13.7 0.7 copy-done.2
  14.4 8.0 %forward.1 = (f32[4,8,128]{2,1,0:T(8,128)S(1)}, bf16[64,4096]{1,0:T(8,128)(2,1)S(1)}, bf16[256,4096]{1,0:T(8,128)(2,1)S(1)}, bf16[256,4096]{1,0:T(8,128)(2,1)S(1...) custom-call(f32[8,16,128]{2,1,0:T(8,128)S(1)} %all-to-all-done.rays_, ...), custom_call_target="tpu_custom_call" | custom-call | tf_op jit(solution)/shard_map/forward/pallas_call | solution.py:520
  22.4 8.4 %all-gather = f32[32,8,128]{2,1,0:T(8,128)S(1)} all-gather(f32[4,8,128]{2,1,0:T(8,128)S(1)} %get-tuple-element.38), channel_id=2, replica_groups=mesh['blk'=8,'rep'=4] {'blk'}, dimensions={0}, use_global_device_ids=true | all-gather | bytes 147456 | tf_op jit(solution)/shard_map/all_gather | solution.py:536
  30.8 3.5 %color.1 = (f32[3,256]{1,0:T(4,128)}, f32[88,256]{1,0:T(8,128)S(1)}, f32[88,256]{1,0:T(8,128)S(1)}, f32[40,1024]{1,0:T(8,128)S(1)}, bf16[256,4096]{1,0:T(8,128)(2,1)S(1)}) custom-call(s32[2,3]{1,0:T(2,128)S(1)} %copy-done.3, s32[1]{0:T(128)} %bitcast.me_ref, f32[8,16,128]{2,1,0:T(8,128)S(1)} %all-to-all-done.rays_ref, f32[8,128]{1,0:T(8,128)S(1)} %copy-done.2, ...), custom_call_target="tpu_custom_call" | custom-call | flops 1207959552 | bytes 2097152 | tf_op jit(solution)/shard_map/color/pallas_call | solution.py:545
  34.4 3.7 %trunk.1 = (f32[144,256]{1,0:T(8,128)S(1)}, f32[144,256]{1,0:T(8,128)S(1)}, f32[144,256]{1,0:T(8,128)S(1)}, f32[144,256]{1,0:T(8,128)S(1)}) custom-call(s32[1]{0:T(128)S(6)} %convert_element_type.3.low_ref, bf16[256,4096]{1,0:T(8,128)(2,1)S(1)} %get-tuple-element.45.d2_ref, bf16[256,4096]{1,0:T(8,128)(2,1)S(1)} %get-tuple-element.46.h1_ref, ...), custom_call_target="tpu_custom_call" | custom-call | flops 4294967296 | bytes 2097152 | tf_op jit(solution)/shard_map/trunk/pallas_call | solution.py:592
  38.1 1.6 %collective-permute-start = (f32[144,256]{1,0:T(8,128)S(1)}, f32[144,256]{1,0:T(8,128)S(1)}, u32[]{:S(2)}, u32[]{:S(2)}) collective-permute-start(f32[144,256]{1,0:T(8,128)S(1)} %get-tuple-element.50), channel_id=1, source_target_pairs={{0,1},{1,0},{2,3},{3,2},{4,5},{5,4},{6,7},{7,6},{8,9},{9,8},{10,11... | collective-permute-start | bytes 442376 | tf_op jit(solution)/shard_map/ppermute | solution.py:594
  40.2 1.6 %collective-permute-start.9 = (f32[40,1024]{1,0:T(8,128)S(1)}, f32[40,1024]{1,0:T(8,128)S(1)}, u32[]{:S(2)}, u32[]{:S(2)}) collective-permute-start(f32[40,1024]{1,0:T(8,128)S(1)} %get-tuple-element.62.own_ref), channel_id=1, source_target_pairs={{0,1},{1,0},{2,3},{3,2},{4,5},{5,4},{6,7},{7,6},{8,9},{9,8},{10,11... | collective-permute-start | bytes 491528 | tf_op jit(solution)/shard_map/ppermute | solution.py:594
  41.8 3.1 %collective-permute-done = f32[144,256]{1,0:T(8,128)S(1)} collective-permute-done((f32[144,256]{1,0:T(8,128)S(1)}, f32[144,256]{1,0:T(8,128)S(1)}, u32[]{:S(2)}, u32[]{:S(2)}) %collective-permute-start) | collective-permute-done | bytes 147488 | tf_op jit(solution)/shard_map/ppermute | solution.py:594
  44.9 3.7 %collective-permute-start.1 = (f32[144,256]{1,0:T(8,128)S(1)}, f32[144,256]{1,0:T(8,128)S(1)}, u32[]{:S(2)}, u32[]{:S(2)}) collective-permute-start(f32[144,256]{1,0:T(8,128)S(1)} %add.18), channel_id=1, source_target_pairs={{0,3},{3,0},{1,2},{2,1},{4,7},{7,4},{5,6},{6,5},{8,11},{11,8},{9,1... | collective-permute-start | bytes 442376 | tf_op jit(solution)/shard_map/ppermute | solution.py:595
  48.6 3.1 %collective-permute-start.4 = (f32[144,256]{1,0:T(8,128)S(1)}, f32[144,256]{1,0:T(8,128)S(1)}, u32[]{:S(2)}, u32[]{:S(2)}) collective-permute-start(f32[144,256]{1,0:T(8,128)S(1)} %add.20), channel_id=1, source_target_pairs={{0,3},{3,0},{1,2},{2,1},{4,7},{7,4},{5,6},{6,5},{8,11},{11,8},{9,1... | collective-permute-start | bytes 442376 | tf_op jit(solution)/shard_map/ppermute | solution.py:595
  51.7 9.2 %collective-permute-done.6 = f32[88,256]{1,0:T(8,128)S(1)} collective-permute-done((f32[88,256]{1,0:T(8,128)S(1)}, f32[88,256]{1,0:T(8,128)S(1)}, u32[]{:S(2)}, u32[]{:S(2)}) %collective-permute-start.6) | collective-permute-done | bytes 90144 | tf_op jit(solution)/shard_map/ppermute | solution.py:594
  60.9 2.0 %collective-permute-start.7 = (f32[88,256]{1,0:T(8,128)S(1)}, f32[88,256]{1,0:T(8,128)S(1)}, u32[]{:S(2)}, u32[]{:S(2)}) collective-permute-start(f32[88,256]{1,0:T(8,128)S(1)} %add.22), channel_id=1, source_target_pairs={{0,3},{3,0},{1,2},{2,1},{4,7},{7,4},{5,6},{6,5},{8,11},{11,8},{9,1... | collective-permute-start | bytes 270344 | tf_op jit(solution)/shard_map/ppermute | solution.py:595
  62.9 1.9 %collective-permute-start.10 = (f32[40,1024]{1,0:T(8,128)S(1)}, f32[40,1024]{1,0:T(8,128)S(1)}, u32[]{:S(2)}, u32[]{:S(2)}) collective-permute-start(f32[40,1024]{1,0:T(8,128)S(1)} %get-tuple-element.62.own_ref), channel_id=1, source_target_pairs={{0,3},{3,0},{1,2},{2,1},{4,7},{7,4},{5,6},{6,5},{8,11},{11,8},{9,1... | collective-permute-start | bytes 491528 | tf_op jit(solution)/shard_map/ppermute | solution.py:595
  64.8 1.9 %collective-permute-start.11 = (f32[40,1024]{1,0:T(8,128)S(1)}, f32[40,1024]{1,0:T(8,128)S(1)}, u32[]{:S(2)}, u32[]{:S(2)}) collective-permute-start(f32[40,1024]{1,0:T(8,128)S(1)} %collective-permute-done.9.near_ref), channel_id=1, source_target_pairs={{0,3},{3,0},{1,2},{2,1},{4,7},{7,4},{5,6},{6,5},{8,11},{11,8},{9,1... | collective-permute-start | bytes 491528 | tf_op jit(solution)/shard_map/ppermute | solution.py:595
  66.9 2.1 %collective-permute-start.5 = (f32[144,256]{1,0:T(8,128)S(1)}, f32[144,256]{1,0:T(8,128)S(1)}, u32[]{:S(2)}, u32[]{:S(2)}) collective-permute-start(f32[144,256]{1,0:T(8,128)S(1)} %add.21.mine0), channel_id=1, source_target_pairs={{0,1},{1,0},{2,3},{3,2},{4,5},{5,4},{6,7},{7,6},{8,9},{9,8},{10,11... | collective-permute-start | bytes 442376 | tf_op jit(solution)/shard_map/ppermute | solution.py:594
  68.9 6.0 %collective-permute-start.8 = (f32[88,256]{1,0:T(8,128)S(1)}, f32[88,256]{1,0:T(8,128)S(1)}, u32[]{:S(2)}, u32[]{:S(2)}) collective-permute-start(f32[88,256]{1,0:T(8,128)S(1)} %add.23.mine), channel_id=1, source_target_pairs={{0,1},{1,0},{2,3},{3,2},{4,5},{5,4},{6,7},{7,6},{8,9},{9,8},{10,11... | collective-permute-start | bytes 270344 | tf_op jit(solution)/shard_map/ppermute | solution.py:594
  74.9 7.7 %collective-permute-done.8.other = f32[88,256]{1,0:T(8,128)S(1)} collective-permute-done((f32[88,256]{1,0:T(8,128)S(1)}, f32[88,256]{1,0:T(8,128)S(1)}, u32[]{:S(2)}, u32[]{:S(2)}) %collective-permute-start.8) | collective-permute-done | bytes 90144 | tf_op jit(solution)/shard_map/ppermute | solution.py:594
  83.3 3.4 %table.1 = f32[32,8192]{1,0:T(8,128)} custom-call(s32[1]{0:T(128)} %bitcast.14.side_ref, f32[40,1024]{1,0:T(8,128)S(1)} %get-tuple-element.62.own_ref, f32[40,1024]{1,0:T(8,128)S(1)} %collective-permute-done.9.near_ref, f32[40,1024]{1,0:T(8,128)S(1)} %collective-permute-done.10.far0_ref, f32[40,1024]{1,0:T(8,128)S(1)} %collective-permute-done.11.far1_ref), custom_call_target="tpu_custom_call" | custom-call | tf_op jit(solution)/shard_map/table/pallas_call | solution.py:624
  86.7 0.8 sides.1
  (25 shorter events, 1.4 us)
Async XLA Ops:
  0.6 30.2 %copy-start.3 = (s32[2,3]{1,0:T(2,128)S(1)}, s32[2,3]{1,0:T(2,128)}, u32[]{:S(2)}) copy-start(s32[2,3]{1,0:T(2,128)} %ids_ref.3) | copy-start | bytes 76
  2.1 10.2 %all-to-all-start = ((f32[8,16,128]{2,1,0:T(8,128)}), f32[8,16,128]{2,1,0:T(8,128)S(1)}, u32[]{:S(2)}, u32[]{:S(2)}) async-start(f32[8,16,128]{2,1,0:T(8,128)} %send.1), calls=%async_computation | async-start | bytes 131072 | tf_op jit(solution)/shard_map/all_to_all | solution.py:478
  12.3 1.4 %copy-start = (bf16[2832,256]{1,0:T(8,128)(2,1)S(1)}, bf16[2832,256]{1,0:T(8,128)(2,1)}, u32[]{:S(2)}) copy-start(bf16[2832,256]{1,0:T(8,128)(2,1)} %get-tuple-element.37.pack_ref) | copy-start | bytes 4349956
  13.7 0.7 copy-start.2
  14.4 16.4 %copy-start.1 = (bf16[2832,256]{1,0:T(8,128)(2,1)S(1)}, bf16[2832,256]{1,0:T(8,128)(2,1)}, u32[]{:S(2)}) copy-start(bf16[2832,256]{1,0:T(8,128)(2,1)} %get-tuple-element.37.pack_ref) | copy-start | bytes 4349956
  38.1 6.8 %collective-permute-start = (f32[144,256]{1,0:T(8,128)S(1)}, f32[144,256]{1,0:T(8,128)S(1)}, u32[]{:S(2)}, u32[]{:S(2)}) collective-permute-start(f32[144,256]{1,0:T(8,128)S(1)} %get-tuple-element.50), channel_id=1, source_target_pairs={{0,1},{1,0},{2,3},{3,2},{4,5},{5,4},{6,7},{7,6},{8,9},{9,8},{10,11... | collective-permute-start | bytes 442376 | tf_op jit(solution)/shard_map/ppermute | solution.py:594
  39.7 8.8 %collective-permute-start.3 = (f32[144,256]{1,0:T(8,128)S(1)}, f32[144,256]{1,0:T(8,128)S(1)}, u32[]{:S(2)}, u32[]{:S(2)}) collective-permute-start(f32[144,256]{1,0:T(8,128)S(1)} %get-tuple-element.52), channel_id=1, source_target_pairs={{0,1},{1,0},{2,3},{3,2},{4,5},{5,4},{6,7},{7,6},{8,9},{9,8},{10,11... | collective-permute-start | bytes 442376 | tf_op jit(solution)/shard_map/ppermute | solution.py:594
  40.2 24.6 %collective-permute-start.9 = (f32[40,1024]{1,0:T(8,128)S(1)}, f32[40,1024]{1,0:T(8,128)S(1)}, u32[]{:S(2)}, u32[]{:S(2)}) collective-permute-start(f32[40,1024]{1,0:T(8,128)S(1)} %get-tuple-element.62.own_ref), channel_id=1, source_target_pairs={{0,1},{1,0},{2,3},{3,2},{4,5},{5,4},{6,7},{7,6},{8,9},{9,8},{10,11... | collective-permute-start | bytes 491528 | tf_op jit(solution)/shard_map/ppermute | solution.py:594
  44.9 21.8 %collective-permute-start.1 = (f32[144,256]{1,0:T(8,128)S(1)}, f32[144,256]{1,0:T(8,128)S(1)}, u32[]{:S(2)}, u32[]{:S(2)}) collective-permute-start(f32[144,256]{1,0:T(8,128)S(1)} %add.18), channel_id=1, source_target_pairs={{0,3},{3,0},{1,2},{2,1},{4,7},{7,4},{5,6},{6,5},{8,11},{11,8},{9,1... | collective-permute-start | bytes 442376 | tf_op jit(solution)/shard_map/ppermute | solution.py:595
  48.6 18.2 %collective-permute-start.4 = (f32[144,256]{1,0:T(8,128)S(1)}, f32[144,256]{1,0:T(8,128)S(1)}, u32[]{:S(2)}, u32[]{:S(2)}) collective-permute-start(f32[144,256]{1,0:T(8,128)S(1)} %add.20), channel_id=1, source_target_pairs={{0,3},{3,0},{1,2},{2,1},{4,7},{7,4},{5,6},{6,5},{8,11},{11,8},{9,1... | collective-permute-start | bytes 442376 | tf_op jit(solution)/shard_map/ppermute | solution.py:595
  51.7 9.2 %collective-permute-start.6 = (f32[88,256]{1,0:T(8,128)S(1)}, f32[88,256]{1,0:T(8,128)S(1)}, u32[]{:S(2)}, u32[]{:S(2)}) collective-permute-start(f32[88,256]{1,0:T(8,128)S(1)} %get-tuple-element.56), channel_id=1, source_target_pairs={{0,1},{1,0},{2,3},{3,2},{4,5},{5,4},{6,7},{7,6},{8,9},{9,8},{10,11... | collective-permute-start | bytes 270344 | tf_op jit(solution)/shard_map/ppermute | solution.py:594
  60.9 8.0 %collective-permute-start.7 = (f32[88,256]{1,0:T(8,128)S(1)}, f32[88,256]{1,0:T(8,128)S(1)}, u32[]{:S(2)}, u32[]{:S(2)}) collective-permute-start(f32[88,256]{1,0:T(8,128)S(1)} %add.22), channel_id=1, source_target_pairs={{0,3},{3,0},{1,2},{2,1},{4,7},{7,4},{5,6},{6,5},{8,11},{11,8},{9,1... | collective-permute-start | bytes 270344 | tf_op jit(solution)/shard_map/ppermute | solution.py:595
  62.9 20.4 %collective-permute-start.10 = (f32[40,1024]{1,0:T(8,128)S(1)}, f32[40,1024]{1,0:T(8,128)S(1)}, u32[]{:S(2)}, u32[]{:S(2)}) collective-permute-start(f32[40,1024]{1,0:T(8,128)S(1)} %get-tuple-element.62.own_ref), channel_id=1, source_target_pairs={{0,3},{3,0},{1,2},{2,1},{4,7},{7,4},{5,6},{6,5},{8,11},{11,8},{9,1... | collective-permute-start | bytes 491528 | tf_op jit(solution)/shard_map/ppermute | solution.py:595
  64.8 18.5 %collective-permute-start.11 = (f32[40,1024]{1,0:T(8,128)S(1)}, f32[40,1024]{1,0:T(8,128)S(1)}, u32[]{:S(2)}, u32[]{:S(2)}) collective-permute-start(f32[40,1024]{1,0:T(8,128)S(1)} %collective-permute-done.9.near_ref), channel_id=1, source_target_pairs={{0,3},{3,0},{1,2},{2,1},{4,7},{7,4},{5,6},{6,5},{8,11},{11,8},{9,1... | collective-permute-start | bytes 491528 | tf_op jit(solution)/shard_map/ppermute | solution.py:595
  66.7 19.9 %collective-permute-start.2 = (f32[144,256]{1,0:T(8,128)S(1)}, f32[144,256]{1,0:T(8,128)S(1)}, u32[]{:S(2)}, u32[]{:S(2)}) collective-permute-start(f32[144,256]{1,0:T(8,128)S(1)} %add.19.mine1), channel_id=1, source_target_pairs={{0,1},{1,0},{2,3},{3,2},{4,5},{5,4},{6,7},{7,6},{8,9},{9,8},{10,11... | collective-permute-start | bytes 442376 | tf_op jit(solution)/shard_map/ppermute | solution.py:594
  66.9 19.8 %collective-permute-start.5 = (f32[144,256]{1,0:T(8,128)S(1)}, f32[144,256]{1,0:T(8,128)S(1)}, u32[]{:S(2)}, u32[]{:S(2)}) collective-permute-start(f32[144,256]{1,0:T(8,128)S(1)} %add.21.mine0), channel_id=1, source_target_pairs={{0,1},{1,0},{2,3},{3,2},{4,5},{5,4},{6,7},{7,6},{8,9},{9,8},{10,11... | collective-permute-start | bytes 442376 | tf_op jit(solution)/shard_map/ppermute | solution.py:594
  68.9 13.7 %collective-permute-start.8 = (f32[88,256]{1,0:T(8,128)S(1)}, f32[88,256]{1,0:T(8,128)S(1)}, u32[]{:S(2)}, u32[]{:S(2)}) collective-permute-start(f32[88,256]{1,0:T(8,128)S(1)} %add.23.mine), channel_id=1, source_target_pairs={{0,1},{1,0},{2,3},{3,2},{4,5},{5,4},{6,7},{7,6},{8,9},{9,8},{10,11... | collective-permute-start | bytes 270344 | tf_op jit(solution)/shard_map/ppermute | solution.py:594
